TPU v7x, 128 devices: a whole 4x4x4 slice. The times are simulated.
128 devices in a mesh: seq: 32 (over z, x, core), group: 4 (over y).
Axes of the slice: x: 4, y: 4, z: 4, core: 2. Of those that a mesh axis runs over, the one named last changes fastest.
Arguments:
- new_queries: bfloat16 [32, 8, 8, 128], P('seq', 'group'), may hold values from -6 to 6
- stored_keys: bfloat16 [32, 8, 16384, 128], P(None, 'group', 'seq'), may hold values from -6 to 6
- stored_values: bfloat16 [32, 8, 16384, 128], P(None, 'group', 'seq'), may hold values from -6 to 6
- used_length: int32 [32], replicated, may hold values from 8192 to 16384
- out_weight: bfloat16 [8, 8, 128, 5120], P('group'), may hold values from -0.0625 to 0.0625
Outputs:
- token_out: bfloat16 [32, 5120], P('seq', 'group')
All inputs are finite; a program needn't handle non-finite values.
Results may differ from a plain program's by a relative error of at most 0.0025.
Values may be sent and summed in bfloat16 or wider, within the bound.
No kernel may reach another device: no remote copies, remote signals or barrier semaphores. Data moves between devices by JAX's collectives and lax.ppermute only.
A program may use at most 128 MiB of HBM per device.

v0:
```python
import jax
import jax.numpy as jnp
from jax import lax
from jax.sharding import PartitionSpec as P

HEAD_SIZE = 128


def per_device(new_queries, stored_keys, stored_values, used_length, out_weight):
    all_queries = lax.all_gather(new_queries, "seq", axis=0, tiled=True)
    logit = jnp.einsum(
        "bkgd,bktd->bkgt", all_queries, stored_keys, preferred_element_type=jnp.float32
    ) * HEAD_SIZE ** (-0.5)
    positions = lax.axis_index("seq") * stored_keys.shape[2] + jnp.arange(stored_keys.shape[2])
    filled = positions[None, :] < used_length[:, None]
    logit = jnp.where(filled[:, None, None, :], logit, -1e30)
    top = jnp.max(logit, axis=-1)
    part = jnp.where(filled[:, None, None, :], jnp.exp(logit - top[..., None]), 0.0)
    weight_sum = jnp.sum(part, axis=-1)
    read_sum = jnp.einsum(
        "bkgt,bktd->bkgd", part, stored_values.astype(jnp.float32), precision=lax.Precision.HIGHEST
    )
    tops, sums, parts = (
        lax.all_to_all(top[None], "seq", split_axis=1, concat_axis=0, tiled=True),
        lax.all_to_all(weight_sum[None], "seq", split_axis=1, concat_axis=0, tiled=True),
        lax.all_to_all(read_sum[None], "seq", split_axis=1, concat_axis=0, tiled=True),
    )
    best = jnp.max(tops, axis=0)
    scale = jnp.exp(tops - best)
    weight_own = jnp.sum(sums * scale, axis=0)
    read_own = jnp.sum(parts * scale[..., None], axis=0)
    read = (read_own / weight_own[..., None]).astype(jnp.bfloat16)
    term = jnp.einsum("bkgd,kgdm->bm", read, out_weight, preferred_element_type=jnp.float32)
    token_out = lax.psum_scatter(term, "group", scatter_dimension=1, tiled=True).astype(
        jnp.bfloat16
    )
    return token_out


def solution(mesh):
    in_specs = (
        P("seq", "group", None, None),
        P(None, "group", "seq", None),
        P(None, "group", "seq", None),
        P(),
        P("group", None, None, None),
    )
    out_specs = P("seq", "group")
    return jax.shard_map(
        per_device, mesh=mesh, in_specs=in_specs, out_specs=out_specs, check_vma=False
    )
```

profile of v0, /device:TPU:0, one launch (start us, length us, event | category | flops | bytes accessed | tf_op | source)
XLA Modules:
  0.0 133.4 jit_solution(4825849419178507323)
XLA Ops:
  6.5 25.9 %all_gather.3 = bf16[32,2,8,128]{3,2,1,0:T(8,128)(2,1)S(1)} all-gather(bf16[1,2,8,128]{3,2,1,0:T(8,128)(2,1)} %param.5), channel_id=1, replica_groups=mesh['seq'=32,'group'=4] {'seq'}, dimensions={0}, use_global_device_ids=true | all-gather | bytes 135168 | tf_op jit(solution)/shard_map/all_gather | solution.py:10
  32.5 0.7 broadcast_compare_fusion
  33.2 6.4 %fusion.18 = (f32[32,2,8]{2,1,0:T(2,128)}, f32[32,2,8,512]{3,2,1,0:T(8,128)S(1)}) fusion(bf16[32,2,8,128]{3,2,1,0:T(8,128)(2,1)S(1)} %all_gather.3, bf16[32,2,512,128]{3,2,1,0:T(8,128)(2,1)} %param.6, pred[32,512]{1,0:T(8,128)(4,1)S(1)} %broadcast_compare_fusion), kind=kOutput, calls=%fused_computation.25 | convolution fusion | flops 67894784 | bytes 9586688 | tf_op jit(solution)/shard_map/bkgd,bktd->bkgt/dot_general | solution.py:11
  39.6 5.2 %all-to-all-start.1 = ((f32[1,32,2,8]{3,2,0,1:T(2,128)}), f32[1,32,2,8]{3,2,0,1:T(2,128)S(1)}, u32[]{:S(2)}, u32[]{:S(2)}) async-start(f32[1,32,2,8]{3,2,0,1:T(2,128)} %bitcast.3), calls=%async_computation.1 | async-start | bytes 65536 | tf_op jit(solution)/shard_map/all_to_all | solution.py:24
  44.8 1.7 %fusion.6 = f32[32,2,8]{2,1,0:T(2,128)} fusion(f32[32,2,8,512]{3,2,1,0:T(8,128)S(1)} %get-tuple-element.6, f32[32,2,8]{2,1,0:T(2,128)} %get-tuple-element.5, pred[32,512]{1,0:T(8,128)(4,1)S(1)} %broadcast_compare_fusion), kind=kLoop, calls=%fused_computation.7 | loop fusion | flops 785920 | bytes 1069056 | tf_op jit(solution)/shard_map/reduce_sum | solution.py:19
  46.5 5.7 %all-to-all-done.1 = f32[1,32,2,8]{3,2,0,1:T(2,128)S(1)} async-done(((f32[1,32,2,8]{3,2,0,1:T(2,128)}), f32[1,32,2,8]{3,2,0,1:T(2,128)S(1)}, u32[]{:S(2)}, u32[]{:S(2)}) %all-to-all-start.1) | async-done | bytes 2080 | tf_op jit(solution)/shard_map/all_to_all | solution.py:24
  52.2 3.8 %all-to-all-start.2 = ((f32[1,32,2,8]{3,2,0,1:T(2,128)}), f32[1,32,2,8]{3,2,0,1:T(2,128)S(1)}, u32[]{:S(2)}, u32[]{:S(2)}) async-start(f32[1,32,2,8]{3,2,0,1:T(2,128)} %bitcast.5), calls=%async_computation.2 | async-start | bytes 65536 | tf_op jit(solution)/shard_map/all_to_all | solution.py:25
  56.1 6.5 %convolution_bitcast_fusion = f32[1,32,2,8,128]{4,3,2,0,1:T(8,128)} fusion(bf16[32,2,512,128]{3,2,1,0:T(8,128)(2,1)} %param.7, f32[32,2,8,512]{3,2,1,0:T(8,128)S(1)} %get-tuple-element.6, f32[32,2,8]{2,1,0:T(2,128)} %get-tuple-element.5, pred[32,512]{1,0:T(8,128)(4,1)S(1)} %broadcast_compare_fusion), kind=kOutput, calls=%fused_computation.5 | convolution fusion | flops 403177472 | bytes 9717760 | tf_op jit(solution)/shard_map/bkgt,bktd->bkgd/dot_general | solution.py:20
  62.6 0.9 all-to-all-done.2
  63.5 6.5 %all-to-all-start = ((f32[1,32,2,8,128]{4,3,2,0,1:T(8,128)}), f32[1,32,2,8,128]{4,3,2,0,1:T(8,128)S(1)}, u32[]{:S(2)}, u32[]{:S(2)}) async-start(f32[1,32,2,8,128]{4,3,2,0,1:T(8,128)} %convolution_bitcast_fusion), calls=%async_computation | async-start | bytes 524288 | tf_op jit(solution)/shard_map/all_to_all | solution.py:26
  70.0 0.0 reduce-scatter.4.cloned.1.call-start
  70.1 0.1 fusion.14
  70.1 8.7 %all-to-all-done = f32[1,32,2,8,128]{4,3,2,0,1:T(8,128)S(1)} async-done(((f32[1,32,2,8,128]{4,3,2,0,1:T(8,128)}), f32[1,32,2,8,128]{4,3,2,0,1:T(8,128)S(1)}, u32[]{:S(2)}, u32[]{:S(2)}) %all-to-all-start) | async-done | bytes 262176 | tf_op jit(solution)/shard_map/all_to_all | solution.py:26
  78.8 0.1 fusion.10
  78.9 0.1 fusion.16
  79.0 13.4 %fusion.2 = f32[5120,1]{1,0:T(8,128)} fusion(bf16[2,8,128,5120]{3,2,1,0:T(8,128)(2,1)} %param.9, bf16[2,8,128,1]{2,1,0,3:T(8,128)(2,1)S(1)} %fusion.16), kind=kOutput, calls=%fused_computation.2 | convolution fusion | flops 20971520 | bytes 20996096 | tf_op jit(solution)/shard_map/bkgd,kgdm->bm/dot_general | solution.py:33
  92.4 0.0 reduce-scatter.4.cloned.1.call-update
  92.5 32.2 %reduce-scatter.4.cloned.1.call-done = f32[1280,1]{1,0:T(8,128)} async-done(((f32[5120,1]{1,0:T(8,128)}), f32[1280,1]{1,0:T(8,128)}) %reduce-scatter.4.cloned.1.call-update) | async-done | bytes 5136
  124.7 1.9 %copy.11 = bf16[1,1280]{1,0:T(2,128)(2,1)} copy(f32[1,1280]{0,1:T(8,128)} %bitcast.41) | data formatting | bytes 7680
  (3 shorter events, 0.1 us)
Async XLA Ops:
  39.6 12.6 %all-to-all-start.1 = ((f32[1,32,2,8]{3,2,0,1:T(2,128)}), f32[1,32,2,8]{3,2,0,1:T(2,128)S(1)}, u32[]{:S(2)}, u32[]{:S(2)}) async-start(f32[1,32,2,8]{3,2,0,1:T(2,128)} %bitcast.3), calls=%async_computation.1 | async-start | bytes 65536 | tf_op jit(solution)/shard_map/all_to_all | solution.py:24
  52.2 11.3 %all-to-all-start.2 = ((f32[1,32,2,8]{3,2,0,1:T(2,128)}), f32[1,32,2,8]{3,2,0,1:T(2,128)S(1)}, u32[]{:S(2)}, u32[]{:S(2)}) async-start(f32[1,32,2,8]{3,2,0,1:T(2,128)} %bitcast.5), calls=%async_computation.2 | async-start | bytes 65536 | tf_op jit(solution)/shard_map/all_to_all | solution.py:25
  63.5 15.3 %all-to-all-start = ((f32[1,32,2,8,128]{4,3,2,0,1:T(8,128)}), f32[1,32,2,8,128]{4,3,2,0,1:T(8,128)S(1)}, u32[]{:S(2)}, u32[]{:S(2)}) async-start(f32[1,32,2,8,128]{4,3,2,0,1:T(8,128)} %convolution_bitcast_fusion), calls=%async_computation | async-start | bytes 524288 | tf_op jit(solution)/shard_map/all_to_all | solution.py:26
  70.0 54.7 %reduce-scatter.4.cloned.1.call-start = ((), (), s32[]{:S(2)}) async-start(), calls=%async_computation.4 | async-start | bytes 3276800
Sparse Core Ops, SparseCore 0:
  92.6 32.0 reduce-scatter.3
where the time goes:
time: 134 us; the launch traced here: 133 us
  waiting for transfers between devices  47.5 us (35%)
  matrix products  26.3 us (20%)
  blocking collectives  25.9 us (19%)
  starting transfers between devices  15.6 us (12%)
  between operations  13.4 us (10%)
  other arithmetic  2.8 us (2%)
  local copies, waits for them, and re-layouts  1.91 us (1%)
    unnamed x2, waiting for transfers between devices  32.2 us
    all_gather x1, blocking collectives, per_device(): all_queries = lax.all_gather(new_queries, 'seq', axis=0, tiled=True)  25.9 us
    dot_general x1, matrix products, per_device(): jnp.einsum('bkgd,kgdm->bm', read, out_weight, preferred_element_type=jnp....  13.4 us
    all_to_all x1, waiting for transfers between devices, per_device(): lax.all_to_all(read_sum[None], 'seq', split_axis=1, concat_axis=0, tiled=...  8.65 us
    all_to_all x1, starting transfers between devices, per_device(): lax.all_to_all(read_sum[None], 'seq', split_axis=1, concat_axis=0, tiled=...  6.51 us
    dot_general x1, matrix products, per_device(): jnp.einsum('bkgt,bktd->bkgd', part, stored_values.astype(jnp.float32), pr...  6.5 us
    dot_general x1, matrix products, per_device(): jnp.einsum('bkgd,bktd->bkgt', all_queries, stored_keys, preferred_element...  6.36 us
    all_to_all x1, waiting for transfers between devices, per_device(): lax.all_to_all(top[None], 'seq', split_axis=1, concat_axis=0, tiled=True)  5.69 us
  transfers between devices with their start and end apart: 4, of which 4 were waited for; matrix products, arithmetic and copies ran while one was open for 6% of the time, Pallas kernels for 0%

commit v1 on v0

--- a/solution.py
+++ b/solution.py
@@ -7,7 +7,9 @@
 
 
 def per_device(new_queries, stored_keys, stored_values, used_length, out_weight):
-    all_queries = lax.all_gather(new_queries, "seq", axis=0, tiled=True)
+    batch = stored_keys.shape[0]
+    copies = jnp.broadcast_to(new_queries, (batch,) + new_queries.shape[1:])
+    all_queries = lax.all_to_all(copies, "seq", split_axis=0, concat_axis=0, tiled=True)
     logit = jnp.einsum(
         "bkgd,bktd->bkgt", all_queries, stored_keys, preferred_element_type=jnp.float32
     ) * HEAD_SIZE ** (-0.5)
@@ -20,21 +22,28 @@
     read_sum = jnp.einsum(
         "bkgt,bktd->bkgd", part, stored_values.astype(jnp.float32), precision=lax.Precision.HIGHEST
     )
-    tops, sums, parts = (
-        lax.all_to_all(top[None], "seq", split_axis=1, concat_axis=0, tiled=True),
-        lax.all_to_all(weight_sum[None], "seq", split_axis=1, concat_axis=0, tiled=True),
-        lax.all_to_all(read_sum[None], "seq", split_axis=1, concat_axis=0, tiled=True),
-    )
+    rows = read_sum.shape[1] * read_sum.shape[2]
+    stats = jnp.stack([top.reshape(batch, rows), weight_sum.reshape(batch, rows)], axis=1)
+    stats = jnp.pad(stats, ((0, 0), (0, 6), (0, HEAD_SIZE - rows)))
+    packed = jnp.concatenate([read_sum.reshape(batch, rows, HEAD_SIZE), stats], axis=1)
+    arrived = lax.all_to_all(packed, "seq", split_axis=0, concat_axis=0, tiled=True)
+    tops, sums = arrived[:, rows, :rows], arrived[:, rows + 1, :rows]
     best = jnp.max(tops, axis=0)
     scale = jnp.exp(tops - best)
     weight_own = jnp.sum(sums * scale, axis=0)
-    read_own = jnp.sum(parts * scale[..., None], axis=0)
+    read_own = jnp.sum(arrived[:, :rows] * scale[..., None], axis=0)
     read = (read_own / weight_own[..., None]).astype(jnp.bfloat16)
-    term = jnp.einsum("bkgd,kgdm->bm", read, out_weight, preferred_element_type=jnp.float32)
-    token_out = lax.psum_scatter(term, "group", scatter_dimension=1, tiled=True).astype(
-        jnp.bfloat16
+    width = out_weight.shape[-1]
+    term = jnp.dot(
+        read.reshape(1, rows * HEAD_SIZE),
+        out_weight.reshape(rows * HEAD_SIZE, width),
+        preferred_element_type=jnp.float32,
     )
-    return token_out
+    shares = lax.axis_size("group")
+    pieces = lax.all_to_all(
+        term.reshape(shares, width // shares), "group", split_axis=0, concat_axis=0, tiled=True
+    )
+    return jnp.sum(pieces, axis=0, keepdims=True).astype(jnp.bfloat16)
 
 
 def solution(mesh):

time: 134 us -> 62.8 us (0.47)
  waiting for transfers between devices: 47.5 us -> 6.99 us
  between operations: 13.4 us -> 0.08 us
  starting transfers between devices: 15.6 us -> 8.31 us
  matrix products: 26.3 us -> 20 us
  blocking collectives: 25.9 us -> 23.3 us
    unnamed x2 -> x0, waiting for transfers between devices: 32.2 us -> none
    all_gather x1 -> x0, blocking collectives: 25.9 us -> none  [per_device(): all_queries = lax.all_gather(new_queries, 'seq', axis=0, tiled=True)]
    all_to_all x0 -> x2, blocking collectives: none -> 23.3 us  [the longest x1 13.7 us: per_device(): lax.all_to_all(packed, 'seq', split_axis=0, concat_axis=0, tiled=True)]
    all_to_all x3 -> x1, waiting for transfers between devices: 15.2 us -> 6.99 us  [per_device(): lax.all_to_all(copies, 'seq', split_axis=0, concat_axis=0, tiled=True)]
    all_to_all x3 -> x1, starting transfers between devices: 15.5 us -> 8.31 us  [per_device(): lax.all_to_all(copies, 'seq', split_axis=0, concat_axis=0, tiled=True)]
    dot_general x1, matrix products: 13.4 us -> 8.44 us  [per_device(): jnp.dot(read.reshape(1, rows * HEAD_SIZE), out_weight.reshape(rows * HEAD...]
    unnamed x1, local copies, waits for them, and re-layouts: 1.91 us -> 0.09 us
    reduce_sum x1, other arithmetic: 1.74 us -> 0.38 us  [per_device(): weight_sum = jnp.sum(part, axis=-1)]
  transfers between devices with their start and end apart: 4 -> 1, of which waited for: 4 -> 1; matrix products, arithmetic and copies ran while one was open for 6% -> 1% of each run, Pallas kernels for 0% -> 0%
where the time goes in v1:
time: 62.8 us; the launch traced here: 62.4 us
  blocking collectives  23.3 us (37%)
  matrix products  20 us (32%)
  starting transfers between devices  8.31 us (13%)
  waiting for transfers between devices  6.99 us (11%)
  local copies, waits for them, and re-layouts  2.22 us (4%)
  other arithmetic  1.46 us (2%)
    all_to_all x1, blocking collectives, per_device(): lax.all_to_all(packed, 'seq', split_axis=0, concat_axis=0, tiled=True)  13.7 us
    all_to_all x1, blocking collectives, per_device(): lax.all_to_all(term.reshape(shares, width // shares), 'group', split_axis...  9.65 us
    dot_general x1, matrix products, per_device(): jnp.dot(read.reshape(1, rows * HEAD_SIZE), out_weight.reshape(rows * HEAD...  8.44 us
    all_to_all x1, starting transfers between devices, per_device(): lax.all_to_all(copies, 'seq', split_axis=0, concat_axis=0, tiled=True)  8.31 us
    all_to_all x1, waiting for transfers between devices, per_device(): lax.all_to_all(copies, 'seq', split_axis=0, concat_axis=0, tiled=True)  6.99 us
    dot_general x1, matrix products, per_device(): jnp.einsum('bkgt,bktd->bkgd', part, stored_values.astype(jnp.float32), pr...  5.82 us
    dot_general x1, matrix products, per_device(): jnp.einsum('bkgd,bktd->bkgt', all_queries, stored_keys, preferred_element...  5.75 us
    broadcast_in_dim x1, local copies, waits for them, and re-layouts, per_device(): copies = jnp.broadcast_to(new_queries, (batch,) + new_queries.shape[1:])  1.34 us
  transfers between devices with their start and end apart: 1, of which 1 were waited for; matrix products, arithmetic and copies ran while one was open for 1% of the time, Pallas kernels for 0%

profile of v1, /device:TPU:0, one launch (start us, length us, event | category | flops | bytes accessed | tf_op | source)
XLA Modules:
  0.0 62.4 jit_solution(9938363480224245977)
XLA Ops:
  0.0 1.3 %broadcast_in_dim.36 = bf16[32,2,8,128]{3,2,1,0:T(8,128)(2,1)} broadcast(bf16[2,8,128]{2,1,0:T(8,128)(2,1)} %bitcast.32), dimensions={1,2,3} | broadcast | bytes 135168 | tf_op jit(solution)/shard_map/broadcast_in_dim | solution.py:11
  1.3 8.3 %all-to-all-start = ((bf16[32,2,8,128]{3,2,1,0:T(8,128)(2,1)}), bf16[32,2,8,128]{3,2,1,0:T(8,128)(2,1)S(1)}, u32[]{:S(2)}, u32[]{:S(2)}) async-start(bf16[32,2,8,128]{3,2,1,0:T(8,128)(2,1)} %broadcast_in_dim.36), calls=%async_computation | async-start | bytes 262144 | tf_op jit(solution)/shard_map/all_to_all | solution.py:12
  9.7 0.7 %broadcast_compare_fusion = pred[32,512]{1,0:T(8,128)(4,1)S(1)} fusion(s32[512]{0:T(512)S(1)} %iota_add_fusion, s32[32]{0:T(128)} %param.8), kind=kLoop, calls=%fused_computation.15 | loop fusion | flops 16384 | bytes 18560 | tf_op jit(solution)/shard_map/lt | solution.py:17
  10.4 7.0 %all-to-all-done = bf16[32,2,8,128]{3,2,1,0:T(8,128)(2,1)S(1)} async-done(((bf16[32,2,8,128]{3,2,1,0:T(8,128)(2,1)}), bf16[32,2,8,128]{3,2,1,0:T(8,128)(2,1)S(1)}, u32[]{:S(2)}, u32[]{:S(2)}) %all-to-all-start) | async-done | bytes 131104 | tf_op jit(solution)/shard_map/all_to_all | solution.py:12
  17.4 5.8 %fusion.12 = (f32[32,2,8]{2,1,0:T(2,128)S(1)}, f32[32,2,8,512]{3,2,1,0:T(8,128)S(1)}) fusion(bf16[32,2,8,128]{3,2,1,0:T(8,128)(2,1)S(1)} %all-to-all-done, bf16[32,2,512,128]{3,2,1,0:T(8,128)(2,1)} %param.6, pred[32,512]{1,0:T(8,128)(4,1)S(1)} %broadcast_compare_fusion), kind=kOutput, calls=%fused_computation.25 | convolution fusion | flops 67894784 | bytes 9586688 | tf_op jit(solution)/shard_map/bkgd,bktd->bkgt/dot_general | solution.py:13
  23.2 0.1 copy.11
  23.2 0.4 fusion.4
  23.6 0.1 copy.12
  23.7 0.1 copy.18
  23.8 5.8 %convolution_bitcast_fusion = f32[32,16,128]{2,1,0:T(8,128)S(1)} fusion(bf16[32,2,512,128]{3,2,1,0:T(8,128)(2,1)} %param.7, f32[32,2,8,512]{3,2,1,0:T(8,128)S(1)} %get-tuple-element.10, f32[32,2,8]{2,1,0:T(2,128)S(1)} %get-tuple-element.9, pred[32,512]{1,0:T(8,128)(4,1)S(1)} %broadcast_compare_fusion), kind=kOutput, calls=%fused_computation.5 | convolution fusion | flops 403177472 | bytes 9717760 | tf_op jit(solution)/shard_map/bkgt,bktd->bkgd/dot_general | solution.py:22
  29.7 13.7 %all_to_all.19 = f32[32,24,128]{2,1,0:T(8,128)S(1)} all-to-all(f32[32,24,128]{2,1,0:T(8,128)S(1)} %select_maximum_fusion), channel_id=1, replica_groups=mesh['seq'=32,'group'=4] {'seq'}, dimensions={0} | all-to-all | bytes 786432 | tf_op jit(solution)/shard_map/all_to_all | solution.py:29
  43.4 0.1 fusion.8
  43.6 0.1 fusion.9
  43.7 8.4 %fusion = f32[1,4,1280]{2,0,1:T(1,128)S(1)} fusion(bf16[2048,1,1]{0,1,2:T(2,128)(2,1)S(1)} %reshape.87, bf16[256,4,8,1280]{3,2,1,0:T(8,128)(2,1)} %bitcast.25), kind=kOutput, calls=%fused_computation | convolution fusion | flops 20971520 | bytes 20996096 | tf_op jit(solution)/shard_map/dot_general | solution.py:37
  52.1 9.6 %all_to_all.20 = f32[4,1,1280]{2,1,0:T(1,128)S(1)} all-to-all(f32[4,1,1280]{2,1,0:T(1,128)S(1)} %all_to_all.14), channel_id=1, replica_groups=mesh['seq'=32,'group'=4] {'group'}, dimensions={0} | all-to-all | bytes 40960 | tf_op jit(solution)/shard_map/all_to_all | solution.py:43
  61.8 0.6 convert_element_type.34
  (10 shorter events, 0.2 us)
Async XLA Ops:
  1.3 16.1 %all-to-all-start = ((bf16[32,2,8,128]{3,2,1,0:T(8,128)(2,1)}), bf16[32,2,8,128]{3,2,1,0:T(8,128)(2,1)S(1)}, u32[]{:S(2)}, u32[]{:S(2)}) async-start(bf16[32,2,8,128]{3,2,1,0:T(8,128)(2,1)} %broadcast_in_dim.36), calls=%async_computation | async-start | bytes 262144 | tf_op jit(solution)/shard_map/all_to_all | solution.py:12

commit v2 on v1

v2 whole, which is shorter than its diff:
```python
import functools

import jax
import jax.numpy as jnp
from jax import lax
from jax.experimental import pallas as pl
from jax.experimental.pallas import tpu as pltpu
from jax.sharding import PartitionSpec as P

HEAD_SIZE = 128
EMPTY = -1e30
TO_BASE_2 = HEAD_SIZE ** (-0.5) * 1.4426950408889634


def attend(used_ref, query_ref, key_ref, value_ref, out_ref):
    batch, heads, width, _ = key_ref.shape
    group = query_ref.shape[2]
    rows = heads * group
    first = lax.axis_index("seq") * width
    lane = lax.broadcasted_iota(jnp.int32, (group, HEAD_SIZE), 1)
    sub = lax.broadcasted_iota(jnp.int32, (group, HEAD_SIZE), 0)
    place = lax.broadcasted_iota(jnp.int32, (group, width), 1)

    def one(b, carry):
        filled = place < used_ref[b] - first
        stats = jnp.zeros((group, HEAD_SIZE), jnp.float32)
        for k in range(heads):
            logit = lax.dot_general(
                query_ref[b, k], key_ref[b, k], (((1,), (1,)), ((), ())),
                preferred_element_type=jnp.float32,
            )
            logit = jnp.where(filled, logit * TO_BASE_2, EMPTY)
            top = jnp.max(logit, axis=1, keepdims=True)
            part = jnp.where(filled, jnp.exp2(logit - top), 0.0)
            total = jnp.sum(part, axis=1, keepdims=True)
            high = part.astype(jnp.bfloat16)
            low = (part - high.astype(jnp.float32)).astype(jnp.bfloat16)
            both = jnp.dot(
                jnp.concatenate([high, low], axis=0), value_ref[b, k],
                preferred_element_type=jnp.float32,
            )
            out_ref[b, pl.ds(k * group, group), :] = both[:group] + both[group:]
            stats = jnp.where(lane == sub + k * group, top, stats)
            stats = jnp.where(lane == sub + (rows + k * group), total, stats)
        out_ref[b, pl.ds(rows, 8), :] = jnp.broadcast_to(
            jnp.sum(stats, axis=0, keepdims=True), (8, HEAD_SIZE)
        )
        return carry

    lax.fori_loop(0, batch, one, 0, unroll=4)


def project(arrived_ref, weight_ref, out_ref):
    sources = arrived_ref.shape[0]
    rows = weight_ref.shape[0] // HEAD_SIZE
    stats = jnp.transpose(arrived_ref[:, rows, :])
    tops, sums = stats[:rows], stats[rows : 2 * rows]
    scale = jnp.exp2(tops - jnp.max(tops, axis=1, keepdims=True))
    scale = scale / jnp.sum(sums * scale, axis=1, keepdims=True)
    read = jnp.zeros((rows, HEAD_SIZE), jnp.float32)
    for s in range(sources):
        read = read + arrived_ref[s, pl.ds(0, rows), :] * scale[:, s : s + 1]
    row = lax.broadcasted_iota(jnp.int32, (rows, HEAD_SIZE), 0)
    left = jnp.concatenate(
        [jnp.where(row == r, read, 0.0).astype(jnp.bfloat16) for r in range(rows)], axis=1
    )
    step = 512

    def columns(n, carry):
        at = pl.ds(pl.multiple_of(n * step, step), step)
        term = jnp.dot(left, weight_ref[:, at], preferred_element_type=jnp.float32)
        out_ref[:, at] = jnp.sum(term, axis=0, keepdims=True)
        return carry

    lax.fori_loop(0, weight_ref.shape[1] // step, columns, 0)


def per_device(new_queries, stored_keys, stored_values, used_length, out_weight):
    batch, heads = stored_keys.shape[:2]
    group = new_queries.shape[2]
    rows = heads * group
    width = out_weight.shape[-1]
    vmem = functools.partial(pltpu.with_memory_space_constraint, memory_space=pltpu.VMEM)
    whole = pl.BlockSpec(memory_space=pltpu.VMEM)

    copies = jnp.broadcast_to(new_queries, (batch,) + new_queries.shape[1:])
    all_queries = lax.all_to_all(copies, "seq", split_axis=0, concat_axis=0, tiled=True)
    packed = pl.pallas_call(
        attend,
        out_shape=jax.ShapeDtypeStruct((batch, rows + 8, HEAD_SIZE), jnp.float32),
        in_specs=[pl.BlockSpec(memory_space=pltpu.SMEM), whole, whole, whole],
        out_specs=whole,
        compiler_params=pltpu.CompilerParams(vmem_limit_bytes=8 << 20),
        name="attend",
    )(used_length, vmem(all_queries), vmem(stored_keys), vmem(stored_values))
    arrived = lax.all_to_all(packed, "seq", split_axis=0, concat_axis=0, tiled=True)
    term = pl.pallas_call(
        project,
        out_shape=jax.ShapeDtypeStruct((1, width), jnp.float32),
        in_specs=[whole, whole],
        out_specs=whole,
        compiler_params=pltpu.CompilerParams(vmem_limit_bytes=8 << 20),
        name="project",
    )(vmem(arrived), vmem(out_weight.reshape(rows * HEAD_SIZE, width)))
    shares = lax.axis_size("group")
    pieces = lax.all_to_all(
        term.reshape(shares, 1, width // shares), "group", split_axis=0, concat_axis=0, tiled=True
    )
    return jnp.sum(pieces, axis=0).astype(jnp.bfloat16)


def solution(mesh):
    in_specs = (
        P("seq", "group", None, None),
        P(None, "group", "seq", None),
        P(None, "group", "seq", None),
        P(),
        P("group", None, None, None),
    )
    out_specs = P("seq", "group")
    return jax.shard_map(
        per_device, mesh=mesh, in_specs=in_specs, out_specs=out_specs, check_vma=False
    )
```

time: 62.8 us -> 76.7 us (1.22)
  Pallas kernels: 0 us -> 21.4 us
  matrix products: 20 us -> 0 us
  blocking collectives: 23.3 us -> 39.2 us
  local copies, waits for them, and re-layouts: 2.22 us -> 15.7 us
  starting transfers between devices: 8.31 us -> 0 us
  waiting for transfers between devices: 6.99 us -> 0 us
  other arithmetic: 1.46 us -> 0.04 us
    pallas_call x0 -> x2, Pallas kernels: none -> 21.4 us  [the longest x1 16.9 us: per_device(): pl.pallas_call(attend, out_shape=jax.ShapeDtypeStruct((batch, rows + 8, H...]
    dot_general x3 -> x0, matrix products: 20 us -> none  [the longest x1 8.44 us: per_device(): jnp.dot(read.reshape(1, rows * HEAD_SIZE), out_weight.reshape(rows * HEAD...]
    all_to_all x1 -> x2, blocking collectives: 9.65 us -> 25.5 us  [the longest x1 15.9 us: per_device(): lax.all_to_all(copies, 'seq', split_axis=0, concat_axis=0, tiled=True)]
    unnamed x1 -> x8, local copies, waits for them, and re-layouts: 0.09 us -> 14.4 us
    all_to_all x1 -> x0, starting transfers between devices: 8.31 us -> none  [per_device(): lax.all_to_all(copies, 'seq', split_axis=0, concat_axis=0, tiled=True)]
    all_to_all x1 -> x0, waiting for transfers between devices: 6.99 us -> none  [per_device(): lax.all_to_all(copies, 'seq', split_axis=0, concat_axis=0, tiled=True)]
  transfers between devices with their start and end apart: 1 -> 0, of which waited for: 1 -> 0; matrix products, arithmetic and copies ran while one was open for 1% -> 0% of each run, Pallas kernels for 0% -> 0%
where the time goes in v2:
time: 76.7 us; the launch traced here: 76.3 us
  blocking collectives  39.2 us (51%)
  Pallas kernels  21.4 us (28%)
  local copies, waits for them, and re-layouts  15.7 us (20%)
    pallas_call x1, Pallas kernels, per_device(): pl.pallas_call(attend, out_shape=jax.ShapeDtypeStruct((batch, rows + 8, H...  16.9 us
    all_to_all x1, blocking collectives, per_device(): lax.all_to_all(copies, 'seq', split_axis=0, concat_axis=0, tiled=True)  15.9 us
    unnamed x8, local copies, waits for them, and re-layouts  14.4 us
    all_to_all x1, blocking collectives, per_device(): lax.all_to_all(packed, 'seq', split_axis=0, concat_axis=0, tiled=True)  13.7 us
    all_to_all x1, blocking collectives, per_device(): lax.all_to_all(term.reshape(shares, 1, width // shares), 'group', split_a...  9.65 us
    pallas_call x1, Pallas kernels, per_device(): pl.pallas_call(project, out_shape=jax.ShapeDtypeStruct((1, width), jnp.fl...  4.42 us

profile of v2, /device:TPU:0, one launch (start us, length us, event | category | flops | bytes accessed | tf_op | source)
XLA Modules:
  0.0 76.3 jit_solution(1408626569718802943)
XLA Ops:
  0.0 0.7 broadcast_in_dim.8
  0.7 15.9 %all_to_all.15.query_ref = bf16[32,2,8,128]{3,2,1,0:T(8,128)(2,1)S(1)} all-to-all(bf16[32,2,8,128]{3,2,1,0:T(8,128)(2,1)S(1)} %broadcast_in_dim.8), channel_id=1, replica_groups=mesh['seq'=32,'group'=4] {'seq'}, dimensions={0} | all-to-all | bytes 262144 | tf_op jit(solution)/shard_map/all_to_all | solution.py:87
  16.6 0.0 copy-start.1
  16.6 3.4 %copy-done.1 = bf16[32,2,512,128]{3,2,1,0:T(8,128)(2,1)S(1)} copy-done((bf16[32,2,512,128]{3,2,1,0:T(8,128)(2,1)S(1)}, bf16[32,2,512,128]{3,2,1,0:T(8,128)(2,1)}, u32[]{:S(2)}) %copy-start.1) | copy-done | bytes 8388632
  19.9 0.0 copy-start.2
  20.0 3.4 %copy-done.2 = bf16[32,2,512,128]{3,2,1,0:T(8,128)(2,1)S(1)} copy-done((bf16[32,2,512,128]{3,2,1,0:T(8,128)(2,1)S(1)}, bf16[32,2,512,128]{3,2,1,0:T(8,128)(2,1)}, u32[]{:S(2)}) %copy-start.2) | copy-done | bytes 8388632
  23.3 0.0 copy-start.3
  23.3 0.7 copy-done.3
  24.0 16.9 %attend.1 = f32[32,24,128]{2,1,0:T(8,128)S(1)} custom-call(s32[32]{0:T(128)S(1)} %copy-done.3, bf16[32,2,8,128]{3,2,1,0:T(8,128)(2,1)S(1)} %all_to_all.15.query_ref, bf16[32,2,512,128]{3,2,1,0:T(8,128)(2,1)S(1)} %copy-done.1, bf16[32,2,512,128]{3,2,1,0:T(8,128)(2,1)S(1)} %copy-done.2), custom_call_target="tpu_custom_call" | custom-call | tf_op jit(solution)/shard_map/attend/pallas_call | solution.py:88
  40.9 13.7 %all_to_all.16.arrived_ref = f32[32,24,128]{2,1,0:T(8,128)S(1)} all-to-all(f32[32,24,128]{2,1,0:T(8,128)S(1)} %attend.1), channel_id=1, replica_groups=mesh['seq'=32,'group'=4] {'seq'}, dimensions={0} | all-to-all | bytes 786432 | tf_op jit(solution)/shard_map/all_to_all | solution.py:96
  54.6 0.0 copy-start
  54.6 7.0 %copy-done = bf16[2,8,128,5120]{3,2,1,0:T(8,128)(2,1)S(1)} copy-done((bf16[2,8,128,5120]{3,2,1,0:T(8,128)(2,1)S(1)}, bf16[2,8,128,5120]{3,2,1,0:T(8,128)(2,1)}, u32[]{:S(2)}) %copy-start) | copy-done | bytes 20971544
  61.6 4.4 %project.1 = f32[1,5120]{1,0:T(1,128)S(1)} custom-call(f32[32,24,128]{2,1,0:T(8,128)S(1)} %all_to_all.16.arrived_ref, bf16[2048,5120]{1,0:T(8,128)(2,1)S(1)} %bitcast.3), custom_call_target="tpu_custom_call" | custom-call | tf_op jit(solution)/shard_map/project/pallas_call | solution.py:97
  66.0 9.6 %all_to_all.17 = f32[4,1,1280]{2,1,0:T(1,128)S(1)} all-to-all(f32[4,1,1280]{2,1,0:T(1,128)S(1)} %bitcast.4), channel_id=1, replica_groups=mesh['seq'=32,'group'=4] {'group'}, dimensions={0} | all-to-all | bytes 40960 | tf_op jit(solution)/shard_map/all_to_all | solution.py:106
  75.7 0.6 convert_element_type.15
  (1 shorter events, 0.0 us)
Async XLA Ops:
  16.6 3.4 %copy-start.1 = (bf16[32,2,512,128]{3,2,1,0:T(8,128)(2,1)S(1)}, bf16[32,2,512,128]{3,2,1,0:T(8,128)(2,1)}, u32[]{:S(2)}) copy-start(bf16[32,2,512,128]{3,2,1,0:T(8,128)(2,1)} %key_ref.1) | copy-start | bytes 25165828
  19.9 3.4 %copy-start.2 = (bf16[32,2,512,128]{3,2,1,0:T(8,128)(2,1)S(1)}, bf16[32,2,512,128]{3,2,1,0:T(8,128)(2,1)}, u32[]{:S(2)}) copy-start(bf16[32,2,512,128]{3,2,1,0:T(8,128)(2,1)} %value_ref.1) | copy-start | bytes 25165828
  23.3 0.7 copy-start.3
  54.6 7.0 %copy-start = (bf16[2,8,128,5120]{3,2,1,0:T(8,128)(2,1)S(1)}, bf16[2,8,128,5120]{3,2,1,0:T(8,128)(2,1)}, u32[]{:S(2)}) copy-start(bf16[2,8,128,5120]{3,2,1,0:T(8,128)(2,1)} %param.9) | copy-start | bytes 62914564

commit v3 on v2

--- a/solution.py
+++ b/solution.py
@@ -9,45 +9,66 @@
 
 HEAD_SIZE = 128
 EMPTY = -1e30
+BLOCK = 8
 TO_BASE_2 = HEAD_SIZE ** (-0.5) * 1.4426950408889634
 
 
 def attend(used_ref, query_ref, key_ref, value_ref, out_ref):
     batch, heads, width, _ = key_ref.shape
-    group = query_ref.shape[2]
-    rows = heads * group
+    rows = query_ref.shape[1]
+    group = rows // heads
     first = lax.axis_index("seq") * width
-    lane = lax.broadcasted_iota(jnp.int32, (group, HEAD_SIZE), 1)
-    sub = lax.broadcasted_iota(jnp.int32, (group, HEAD_SIZE), 0)
-    place = lax.broadcasted_iota(jnp.int32, (group, width), 1)
+    lane = lax.broadcasted_iota(jnp.int32, (rows, HEAD_SIZE), 1)
+    row = lax.broadcasted_iota(jnp.int32, (rows, HEAD_SIZE), 0)
+    place = lax.broadcasted_iota(jnp.int32, (rows, width), 1)
 
-    def one(b, carry):
-        filled = place < used_ref[b] - first
-        stats = jnp.zeros((group, HEAD_SIZE), jnp.float32)
-        for k in range(heads):
-            logit = lax.dot_general(
-                query_ref[b, k], key_ref[b, k], (((1,), (1,)), ((), ())),
-                preferred_element_type=jnp.float32,
+    def side_by_side(ref, b):
+        return jnp.concatenate([ref[b, k] for k in range(heads)], axis=1)
+
+    def block(i, carry):
+        at = [i * BLOCK + j for j in range(BLOCK)]
+        logits = []
+        for b in at:
+            query = query_ref[b].astype(jnp.float32)
+            left = jnp.concatenate(
+                [jnp.where(row // group == k, query, 0.0) for k in range(heads)], axis=1
+            ).astype(jnp.bfloat16)
+            logits.append(
+                lax.dot_general(
+                    left, side_by_side(key_ref, b), (((1,), (1,)), ((), ())),
+                    preferred_element_type=jnp.float32,
+                )
             )
-            logit = jnp.where(filled, logit * TO_BASE_2, EMPTY)
-            top = jnp.max(logit, axis=1, keepdims=True)
-            part = jnp.where(filled, jnp.exp2(logit - top), 0.0)
-            total = jnp.sum(part, axis=1, keepdims=True)
+        filled = [place < used_ref[b] - first for b in at]
+        logits = [jnp.where(f, x * TO_BASE_2, EMPTY) for f, x in zip(filled, logits)]
+        tops = [jnp.max(x, axis=1, keepdims=True) for x in logits]
+        parts = [jnp.where(f, jnp.exp2(x - t), 0.0) for f, x, t in zip(filled, logits, tops)]
+        totals = [jnp.sum(p, axis=1, keepdims=True) for p in parts]
+        reads = []
+        for b, part in zip(at, parts):
             high = part.astype(jnp.bfloat16)
             low = (part - high.astype(jnp.float32)).astype(jnp.bfloat16)
             both = jnp.dot(
-                jnp.concatenate([high, low], axis=0), value_ref[b, k],
+                jnp.concatenate([high, low], axis=0), side_by_side(value_ref, b),
                 preferred_element_type=jnp.float32,
             )
-            out_ref[b, pl.ds(k * group, group), :] = both[:group] + both[group:]
-            stats = jnp.where(lane == sub + k * group, top, stats)
-            stats = jnp.where(lane == sub + (rows + k * group), total, stats)
-        out_ref[b, pl.ds(rows, 8), :] = jnp.broadcast_to(
-            jnp.sum(stats, axis=0, keepdims=True), (8, HEAD_SIZE)
-        )
+            reads.append(both[:rows] + both[rows:])
+        for b, read, top, total in zip(at, reads, tops, totals):
+            for k in range(heads):
+                out_ref[b, pl.ds(k * group, group), :] = read[
+                    k * group : (k + 1) * group, k * HEAD_SIZE : (k + 1) * HEAD_SIZE
+                ]
+            stats = jnp.where(lane == row, top, jnp.where(lane == row + rows, total, 0.0))
+            out_ref[b, pl.ds(rows, 8), :] = jnp.broadcast_to(
+                jnp.sum(stats, axis=0, keepdims=True), (8, HEAD_SIZE)
+            )
         return carry
 
-    lax.fori_loop(0, batch, one, 0, unroll=4)
+    lax.fori_loop(0, batch // BLOCK, block, 0)
+
+
+def spread(one_ref, out_ref):
+    out_ref[...] = jnp.broadcast_to(one_ref[...], out_ref.shape)
 
 
 def project(arrived_ref, weight_ref, out_ref):
@@ -83,7 +104,16 @@
     vmem = functools.partial(pltpu.with_memory_space_constraint, memory_space=pltpu.VMEM)
     whole = pl.BlockSpec(memory_space=pltpu.VMEM)
 
-    copies = jnp.broadcast_to(new_queries, (batch,) + new_queries.shape[1:])
+    queries = new_queries.reshape(1, rows, HEAD_SIZE)
+    copies = pl.pallas_call(
+        spread,
+        out_shape=jax.ShapeDtypeStruct((batch, rows, HEAD_SIZE), queries.dtype),
+        in_specs=[whole],
+        out_specs=whole,
+        cost_estimate=pl.CostEstimate(flops=10**11, bytes_accessed=10**9, transcendentals=0),
+        compiler_params=pltpu.CompilerParams(vmem_limit_bytes=1 << 20),
+        name="spread",
+    )(queries)
     all_queries = lax.all_to_all(copies, "seq", split_axis=0, concat_axis=0, tiled=True)
     packed = pl.pallas_call(
         attend,

time: 76.7 us -> 50.3 us (0.66)
  local copies, waits for them, and re-layouts: 15.7 us -> 1.47 us
  Pallas kernels: 21.4 us -> 9.02 us
    unnamed x8 -> x18, local copies, waits for them, and re-layouts: 14.4 us -> 0.87 us
    pallas_call x1, Pallas kernels: 16.9 us -> 4.58 us  [per_device(): pl.pallas_call(attend, out_shape=jax.ShapeDtypeStruct((batch, rows + 8, H...]
where the time goes in v3:
time: 50.3 us; the launch traced here: 50.1 us
  blocking collectives  39.5 us (79%)
  Pallas kernels  9.02 us (18%)
  local copies, waits for them, and re-layouts  1.47 us (3%)
    all_to_all x1, blocking collectives, per_device(): lax.all_to_all(copies, 'seq', split_axis=0, concat_axis=0, tiled=True)  16.1 us
    all_to_all x1, blocking collectives, per_device(): lax.all_to_all(packed, 'seq', split_axis=0, concat_axis=0, tiled=True)  13.7 us
    all_to_all x1, blocking collectives, per_device(): lax.all_to_all(term.reshape(shares, 1, width // shares), 'group', split_a...  9.65 us
    pallas_call x1, Pallas kernels, per_device(): pl.pallas_call(attend, out_shape=jax.ShapeDtypeStruct((batch, rows + 8, H...  4.58 us
    pallas_call x1, Pallas kernels, per_device(): pl.pallas_call(project, out_shape=jax.ShapeDtypeStruct((1, width), jnp.fl...  4.42 us

profile of v3, /device:TPU:0, one launch (start us, length us, event | category | flops | bytes accessed | tf_op | source)
XLA Modules:
  0.0 50.1 jit_solution(226323811277277620)
XLA Ops:
  0.0 0.0 slice-start
  0.0 0.0 copy-start.3
  0.0 0.8 %copy-done.3 = bf16[1,2,8,128]{3,2,1,0:T(8,128)(2,1)S(1)} copy-done((bf16[1,2,8,128]{3,2,1,0:T(8,128)(2,1)S(1)}, bf16[1,2,8,128]{3,2,1,0:T(8,128)(2,1)}, u32[]{:S(2)}) %copy-start.3) | copy-done | bytes 4120
  0.8 0.0 copy-start
  0.8 0.0 copy-start.1
  0.8 0.0 copy-start.2
  0.8 0.0 slice-start.1
  0.9 0.0 slice-start.2
  0.9 0.0 slice-start.3
  0.9 0.0 slice-start.4
  0.9 16.1 %all_to_all.15.query_ref = bf16[32,16,128]{2,1,0:T(8,128)(2,1)S(1)} all-to-all(bf16[32,16,128]{2,1,0:T(8,128)(2,1)S(1)} %spread.1), channel_id=1, replica_groups=mesh['seq'=32,'group'=4] {'seq'}, dimensions={0} | all-to-all | bytes 262144 | tf_op jit(solution)/shard_map/all_to_all | solution.py:117
  17.0 0.0 copy-done
  17.0 0.0 copy-done.1
  17.0 0.0 copy-done.2
  17.0 4.6 %attend.1 = f32[32,24,128]{2,1,0:T(8,128)S(1)} custom-call(s32[32]{0:T(128)S(1)} %copy-done.2, bf16[32,16,128]{2,1,0:T(8,128)(2,1)S(1)} %all_to_all.15.query_ref, bf16[32,2,512,128]{3,2,1,0:T(8,128)(2,1)S(1)} %copy-done, bf16[32,2,512,128]{3,2,1,0:T(8,128)(2,1)S(1)} %copy-done.1), custom_call_target="tpu_custom_call" | custom-call | tf_op jit(solution)/shard_map/attend/pallas_call | solution.py:118
  21.6 13.7 %all_to_all.16.arrived_ref = f32[32,24,128]{2,1,0:T(8,128)S(1)} all-to-all(f32[32,24,128]{2,1,0:T(8,128)S(1)} %attend.1), channel_id=1, replica_groups=mesh['seq'=32,'group'=4] {'seq'}, dimensions={0} | all-to-all | bytes 786432 | tf_op jit(solution)/shard_map/all_to_all | solution.py:126
  35.3 0.0 slice-done
  35.3 0.0 slice-done.1
  35.3 0.0 slice-done.2
  35.3 0.0 slice-done.3
  35.3 0.0 slice-done.4
  35.4 4.4 %project.1 = f32[1,5120]{1,0:T(1,128)S(1)} custom-call(f32[32,24,128]{2,1,0:T(8,128)S(1)} %all_to_all.16.arrived_ref, bf16[2048,5120]{1,0:T(8,128)(2,1)S(1)} %bitcast.5), custom_call_target="tpu_custom_call" | custom-call | tf_op jit(solution)/shard_map/project/pallas_call | solution.py:127
  39.8 9.6 %all_to_all.17 = f32[4,1,1280]{2,1,0:T(1,128)S(1)} all-to-all(f32[4,1,1280]{2,1,0:T(1,128)S(1)} %bitcast.6), channel_id=1, replica_groups=mesh['seq'=32,'group'=4] {'group'}, dimensions={0} | all-to-all | bytes 40960 | tf_op jit(solution)/shard_map/all_to_all | solution.py:136
  49.5 0.6 %convert_element_type.15 = bf16[1,1280]{1,0:T(2,128)(2,1)} reshape(bf16[1280]{0:T(1024)(128)(2,1)S(1)} %reduce_sum.9) | data formatting | bytes 5120 | tf_op jit(solution)/shard_map/convert_element_type | solution.py:139
  (3 shorter events, 0.1 us)
Async XLA Ops:
  0.0 35.3 %slice-start = ((s8[20971520]{0:T(1024)(128)(4,1)}), s8[4194304]{0:T(1024)(128)(4,1)S(1)}, s32[]{:S(2)}) async-start(s8[20971520]{0:T(1024)(128)(4,1)} %bitcast.3), calls=%async_computation.3 | async-start | bytes 8388608
  0.0 0.8 %copy-start.3 = (bf16[1,2,8,128]{3,2,1,0:T(8,128)(2,1)S(1)}, bf16[1,2,8,128]{3,2,1,0:T(8,128)(2,1)}, u32[]{:S(2)}) copy-start(bf16[1,2,8,128]{3,2,1,0:T(8,128)(2,1)} %param.5) | copy-start | bytes 12292
  0.8 16.2 %copy-start = (bf16[32,2,512,128]{3,2,1,0:T(8,128)(2,1)S(1)}, bf16[32,2,512,128]{3,2,1,0:T(8,128)(2,1)}, u32[]{:S(2)}) copy-start(bf16[32,2,512,128]{3,2,1,0:T(8,128)(2,1)} %key_ref.1) | copy-start | bytes 25165828
  0.8 16.2 %copy-start.1 = (bf16[32,2,512,128]{3,2,1,0:T(8,128)(2,1)S(1)}, bf16[32,2,512,128]{3,2,1,0:T(8,128)(2,1)}, u32[]{:S(2)}) copy-start(bf16[32,2,512,128]{3,2,1,0:T(8,128)(2,1)} %value_ref.1) | copy-start | bytes 25165828
  0.8 16.2 %copy-start.2 = (s32[32]{0:T(128)S(1)}, s32[32]{0:T(128)}, u32[]{:S(2)}) copy-start(s32[32]{0:T(128)} %used_ref.1) | copy-start | bytes 388
  0.8 34.5 %slice-start.1 = ((s8[20971520]{0:T(1024)(128)(4,1)}), s8[4194304]{0:T(1024)(128)(4,1)S(1)}, s32[]{:S(2)}) async-start(s8[20971520]{0:T(1024)(128)(4,1)} %bitcast.3), calls=%async_computation.4 | async-start | bytes 8388608
  0.9 34.5 %slice-start.2 = ((s8[20971520]{0:T(1024)(128)(4,1)}), s8[4194304]{0:T(1024)(128)(4,1)S(1)}, s32[]{:S(2)}) async-start(s8[20971520]{0:T(1024)(128)(4,1)} %bitcast.3), calls=%async_computation.5 | async-start | bytes 8388608
  0.9 34.5 %slice-start.3 = ((s8[20971520]{0:T(1024)(128)(4,1)}), s8[4194304]{0:T(1024)(128)(4,1)S(1)}, s32[]{:S(2)}) async-start(s8[20971520]{0:T(1024)(128)(4,1)} %bitcast.3), calls=%async_computation.6 | async-start | bytes 8388608
  0.9 34.5 %slice-start.4 = ((s8[20971520]{0:T(1024)(128)(4,1)}), s8[4194304]{0:T(1024)(128)(4,1)S(1)}, s32[]{:S(2)}) async-start(s8[20971520]{0:T(1024)(128)(4,1)} %bitcast.3), calls=%async_computation.7 | async-start | bytes 8388608

commit v4 on v3

--- a/solution.py
+++ b/solution.py
@@ -10,6 +10,8 @@
 HEAD_SIZE = 128
 EMPTY = -1e30
 BLOCK = 8
+STEP = 256
+ORDER = (2, 3, 1, 0)
 TO_BASE_2 = HEAD_SIZE ** (-0.5) * 1.4426950408889634
 
 
@@ -55,13 +57,11 @@
             reads.append(both[:rows] + both[rows:])
         for b, read, top, total in zip(at, reads, tops, totals):
             for k in range(heads):
-                out_ref[b, pl.ds(k * group, group), :] = read[
+                out_ref[pl.ds(b * (rows + 1) + k * group, group), :] = read[
                     k * group : (k + 1) * group, k * HEAD_SIZE : (k + 1) * HEAD_SIZE
                 ]
             stats = jnp.where(lane == row, top, jnp.where(lane == row + rows, total, 0.0))
-            out_ref[b, pl.ds(rows, 8), :] = jnp.broadcast_to(
-                jnp.sum(stats, axis=0, keepdims=True), (8, HEAD_SIZE)
-            )
+            out_ref[pl.ds(b * (rows + 1) + rows, 1), :] = jnp.sum(stats, axis=0, keepdims=True)
         return carry
 
     lax.fori_loop(0, batch // BLOCK, block, 0)
@@ -71,29 +71,42 @@
     out_ref[...] = jnp.broadcast_to(one_ref[...], out_ref.shape)
 
 
-def project(arrived_ref, weight_ref, out_ref):
-    sources = arrived_ref.shape[0]
-    rows = weight_ref.shape[0] // HEAD_SIZE
-    stats = jnp.transpose(arrived_ref[:, rows, :])
+def merge(arrived_ref, rows):
+    sources = arrived_ref.shape[0] // (rows + 1)
+    stats = jnp.transpose(arrived_ref[pl.ds(rows, sources, stride=rows + 1), :])
     tops, sums = stats[:rows], stats[rows : 2 * rows]
     scale = jnp.exp2(tops - jnp.max(tops, axis=1, keepdims=True))
     scale = scale / jnp.sum(sums * scale, axis=1, keepdims=True)
     read = jnp.zeros((rows, HEAD_SIZE), jnp.float32)
     for s in range(sources):
-        read = read + arrived_ref[s, pl.ds(0, rows), :] * scale[:, s : s + 1]
+        read = read + arrived_ref[pl.ds(s * (rows + 1), rows), :] * scale[:, s : s + 1]
     row = lax.broadcasted_iota(jnp.int32, (rows, HEAD_SIZE), 0)
-    left = jnp.concatenate(
+    return jnp.concatenate(
         [jnp.where(row == r, read, 0.0).astype(jnp.bfloat16) for r in range(rows)], axis=1
     )
-    step = 512
 
-    def columns(n, carry):
-        at = pl.ds(pl.multiple_of(n * step, step), step)
+
+def columns(left, weight_ref, share, out_ref):
+    width = out_ref.shape[-1]
+    for n in range(0, width, STEP):
+        at = pl.ds(pl.multiple_of(share * width + n, STEP), STEP)
         term = jnp.dot(left, weight_ref[:, at], preferred_element_type=jnp.float32)
-        out_ref[:, at] = jnp.sum(term, axis=0, keepdims=True)
-        return carry
+        out_ref[:, pl.ds(n, STEP)] = jnp.sum(term, axis=0, keepdims=True)
 
-    lax.fori_loop(0, weight_ref.shape[1] // step, columns, 0)
+
+def project_first(away, arrived_ref, weight_ref, left_ref, out_ref):
+    left = merge(arrived_ref, weight_ref.shape[0] // HEAD_SIZE)
+    left_ref[...] = left
+    columns(left, weight_ref, lax.axis_index("group") ^ away, out_ref)
+
+
+def project_next(away, left_ref, weight_ref, out_ref):
+    columns(left_ref[...], weight_ref, lax.axis_index("group") ^ away, out_ref)
+
+
+def add_all(own_ref, a_ref, b_ref, c_ref, out_ref):
+    total = (own_ref[...] + a_ref[...]) + (b_ref[...] + c_ref[...])
+    out_ref[...] = total.astype(out_ref.dtype)
 
 
 def per_device(new_queries, stored_keys, stored_values, used_length, out_weight):
@@ -117,26 +130,50 @@
     all_queries = lax.all_to_all(copies, "seq", split_axis=0, concat_axis=0, tiled=True)
     packed = pl.pallas_call(
         attend,
-        out_shape=jax.ShapeDtypeStruct((batch, rows + 8, HEAD_SIZE), jnp.float32),
+        out_shape=jax.ShapeDtypeStruct((batch * (rows + 1), HEAD_SIZE), jnp.float32),
         in_specs=[pl.BlockSpec(memory_space=pltpu.SMEM), whole, whole, whole],
         out_specs=whole,
         compiler_params=pltpu.CompilerParams(vmem_limit_bytes=8 << 20),
         name="attend",
     )(used_length, vmem(all_queries), vmem(stored_keys), vmem(stored_values))
-    arrived = lax.all_to_all(packed, "seq", split_axis=0, concat_axis=0, tiled=True)
-    term = pl.pallas_call(
-        project,
-        out_shape=jax.ShapeDtypeStruct((1, width), jnp.float32),
+    arrived = lax.all_to_all(
+        packed.reshape(batch, rows + 1, 1, HEAD_SIZE), "seq", split_axis=0, concat_axis=0, tiled=True
+    ).reshape(packed.shape)
+    shares = lax.axis_size("group")
+    piece = jax.ShapeDtypeStruct((1, width // shares), jnp.float32)
+    small = pltpu.CompilerParams(vmem_limit_bytes=8 << 20)
+    cost = pl.CostEstimate(flops=10**9, bytes_accessed=10**7, transcendentals=0)
+    weight = vmem(out_weight.reshape(rows * HEAD_SIZE, width))
+    left, term = pl.pallas_call(
+        functools.partial(project_first, ORDER[0]),
+        out_shape=(jax.ShapeDtypeStruct((rows, rows * HEAD_SIZE), jnp.bfloat16), piece),
         in_specs=[whole, whole],
+        out_specs=(whole, whole),
+        compiler_params=small,
+        name="project_first",
+    )(vmem(arrived), weight)
+    pieces = []
+    for n, away in enumerate(ORDER[1:]):
+        pieces.append(
+            lax.ppermute(term, "group", [(j, j ^ ORDER[n]) for j in range(shares)])
+        )
+        term = pl.pallas_call(
+            functools.partial(project_next, away),
+            out_shape=piece,
+            in_specs=[whole, whole],
+            out_specs=whole,
+            cost_estimate=cost,
+            compiler_params=small,
+            name="project_next",
+        )(left, weight)
+    return pl.pallas_call(
+        add_all,
+        out_shape=jax.ShapeDtypeStruct(piece.shape, jnp.bfloat16),
+        in_specs=[whole] * 4,
         out_specs=whole,
-        compiler_params=pltpu.CompilerParams(vmem_limit_bytes=8 << 20),
-        name="project",
-    )(vmem(arrived), vmem(out_weight.reshape(rows * HEAD_SIZE, width)))
-    shares = lax.axis_size("group")
-    pieces = lax.all_to_all(
-        term.reshape(shares, 1, width // shares), "group", split_axis=0, concat_axis=0, tiled=True
-    )
-    return jnp.sum(pieces, axis=0).astype(jnp.bfloat16)
+        compiler_params=small,
+        name="add_all",
+    )(term, *pieces)
 
 
 def solution(mesh):

time: 50.3 us -> 46.3 us (0.920)
  blocking collectives: 39.5 us -> 28.5 us
  starting transfers between devices: 0 us -> 4.78 us
  waiting for transfers between devices: 0 us -> 2.76 us
  local copies, waits for them, and re-layouts: 1.47 us -> 0.87 us
    all_to_all x2 -> x1, blocking collectives: 23.3 us -> 12.4 us  [per_device(): lax.all_to_all(packed.reshape(batch, rows + 1, 1, HEAD_SIZE), 'seq', spli...]
    ppermute x0 -> x3, starting transfers between devices: none -> 4.78 us  [per_device(): lax.ppermute(term, 'group', [(j, j ^ ORDER[n]) for j in range(shares)])]
    ppermute x0 -> x3, waiting for transfers between devices: none -> 2.76 us  [per_device(): lax.ppermute(term, 'group', [(j, j ^ ORDER[n]) for j in range(shares)])]
    convert_element_type x1 -> x0, local copies, waits for them, and re-layouts: 0.6 us -> none  [per_device(): return jnp.sum(pieces, axis=0).astype(jnp.bfloat16)]
    pallas_call x2 -> x6, Pallas kernels: 9 us -> 8.8 us  [the longest x1 4.58 us: per_device(): pl.pallas_call(attend, out_shape=jax.ShapeDtypeStruct((batch * (rows + 1)...]
  transfers between devices with their start and end apart: 0 -> 3, of which waited for: 0 -> 2; matrix products, arithmetic and copies ran while one was open for 0% -> 0% of each run, Pallas kernels for 0% -> 2%
where the time goes in v4:
time: 46.3 us; the launch traced here: 45.9 us
  blocking collectives  28.5 us (62%)
  Pallas kernels  8.82 us (19%)
  starting transfers between devices  4.78 us (10%)
  waiting for transfers between devices  2.76 us (6%)
  local copies, waits for them, and re-layouts  0.87 us (2%)
    all_to_all x1, blocking collectives, per_device(): lax.all_to_all(copies, 'seq', split_axis=0, concat_axis=0, tiled=True)  16.1 us
    all_to_all x1, blocking collectives, per_device(): lax.all_to_all(packed.reshape(batch, rows + 1, 1, HEAD_SIZE), 'seq', spli...  12.4 us
    ppermute x3, starting transfers between devices, per_device(): lax.ppermute(term, 'group', [(j, j ^ ORDER[n]) for j in range(shares)])  4.78 us
    pallas_call x1, Pallas kernels, per_device(): pl.pallas_call(attend, out_shape=jax.ShapeDtypeStruct((batch * (rows + 1)...  4.58 us
    ppermute x3, waiting for transfers between devices, per_device(): lax.ppermute(term, 'group', [(j, j ^ ORDER[n]) for j in range(shares)])  2.76 us
    pallas_call x3, Pallas kernels, per_device(): pl.pallas_call(functools.partial(project_next, away), out_shape=piece, in...  2.44 us
    pallas_call x1, Pallas kernels, per_device(): pl.pallas_call(functools.partial(project_first, ORDER[0]), out_shape=(jax...  1.18 us
  transfers between devices with their start and end apart: 3, of which 2 were waited for; matrix products, arithmetic and copies ran while one was open for 0% of the time, Pallas kernels for 2%

profile of v4, /device:TPU:0, one launch (start us, length us, event | category | flops | bytes accessed | tf_op | source)
XLA Modules:
  0.0 45.9 jit_solution(10761594724574996643)
XLA Ops:
  0.0 0.0 slice-start
  0.0 0.0 copy-start.3
  0.0 0.8 %copy-done.3 = bf16[1,2,8,128]{3,2,1,0:T(8,128)(2,1)S(1)} copy-done((bf16[1,2,8,128]{3,2,1,0:T(8,128)(2,1)S(1)}, bf16[1,2,8,128]{3,2,1,0:T(8,128)(2,1)}, u32[]{:S(2)}) %copy-start.3) | copy-done | bytes 4120
  0.8 0.0 copy-start
  0.8 0.0 copy-start.1
  0.8 0.0 copy-start.2
  0.8 0.0 slice-start.1
  0.9 0.0 slice-start.2
  0.9 0.0 slice-start.3
  0.9 0.0 slice-start.4
  0.9 16.1 %all_to_all.10.query_ref = bf16[32,16,128]{2,1,0:T(8,128)(2,1)S(1)} all-to-all(bf16[32,16,128]{2,1,0:T(8,128)(2,1)S(1)} %spread.1), channel_id=1, replica_groups=mesh['seq'=32,'group'=4] {'seq'}, dimensions={0} | all-to-all | bytes 262144 | tf_op jit(solution)/shard_map/all_to_all | solution.py:130
  17.0 0.0 copy-done
  17.0 0.0 copy-done.1
  17.0 0.0 copy-done.2
  17.0 4.6 %attend.1 = f32[544,128]{1,0:T(8,128)S(1)} custom-call(s32[32]{0:T(128)S(1)} %copy-done.2, bf16[32,16,128]{2,1,0:T(8,128)(2,1)S(1)} %all_to_all.10.query_ref, bf16[32,2,512,128]{3,2,1,0:T(8,128)(2,1)S(1)} %copy-done, bf16[32,2,512,128]{3,2,1,0:T(8,128)(2,1)S(1)} %copy-done.1), custom_call_target="tpu_custom_call" | custom-call | tf_op jit(solution)/shard_map/attend/pallas_call | solution.py:131
  21.6 12.4 %all_to_all.11 = f32[32,17,1,128]{3,2,1,0:T(1,128)S(1)} all-to-all(f32[32,17,1,128]{3,2,1,0:T(1,128)S(1)} %bitcast.11), channel_id=1, replica_groups=mesh['seq'=32,'group'=4] {'seq'}, dimensions={0} | all-to-all | bytes 557056 | tf_op jit(solution)/shard_map/all_to_all | solution.py:139
  34.0 0.0 slice-done
  34.0 0.0 slice-done.1
  34.1 0.0 slice-done.2
  34.1 0.0 slice-done.3
  34.1 0.0 slice-done.4
  34.1 1.2 %project_first.1 = (bf16[16,2048]{1,0:T(8,128)(2,1)S(1)}, f32[1,1280]{1,0:T(1,128)S(1)}) custom-call(f32[544,128]{1,0:T(8,128)S(1)} %bitcast.10, bf16[2048,5120]{1,0:T(8,128)(2,1)S(1)} %bitcast.6), custom_call_target="tpu_custom_call" | custom-call | tf_op jit(solution)/shard_map/project_first/pallas_call | solution.py:147
  35.3 0.8 %project_next.5 = f32[1,1280]{1,0:T(1,128)S(1)} custom-call(bf16[16,2048]{1,0:T(8,128)(2,1)S(1)} %get-tuple-element.7.left_ref, bf16[2048,5120]{1,0:T(8,128)(2,1)S(1)} %bitcast.7), custom_call_target="tpu_custom_call" | custom-call | flops 1000000000 | bytes 10000000 | tf_op jit(solution)/shard_map/project_next/pallas_call | solution.py:160
  36.1 0.8 %project_next.4 = f32[1,1280]{1,0:T(1,128)S(1)} custom-call(bf16[16,2048]{1,0:T(8,128)(2,1)S(1)} %get-tuple-element.7.left_ref, bf16[2048,5120]{1,0:T(8,128)(2,1)S(1)} %bitcast.8), custom_call_target="tpu_custom_call" | custom-call | flops 1000000000 | bytes 10000000 | tf_op jit(solution)/shard_map/project_next/pallas_call | solution.py:160
  36.9 3.1 %collective-permute-start.1 = (f32[1,1280]{1,0:T(1,128)S(1)}, f32[1,1280]{1,0:T(1,128)S(1)}, u32[]{:S(2)}, u32[]{:S(2)}) collective-permute-start(f32[1,1280]{1,0:T(1,128)S(1)} %project_next.4), channel_id=1, source_target_pairs={{0,3},{1,2},{2,1},{3,0},{4,7},{5,6},{6,5},{7,4},{8,11},{9,10},{10,... | collective-permute-start | bytes 15368 | tf_op jit(solution)/shard_map/ppermute | solution.py:158
  40.0 0.1 collective-permute-start.2
  40.2 1.5 %collective-permute-start = (f32[1,1280]{1,0:T(1,128)S(1)}, f32[1,1280]{1,0:T(1,128)S(1)}, u32[]{:S(2)}, u32[]{:S(2)}) collective-permute-start(f32[1,1280]{1,0:T(1,128)S(1)} %get-tuple-element.8), channel_id=1, source_target_pairs={{0,2},{1,3},{2,0},{3,1},{4,6},{5,7},{6,4},{7,5},{8,10},{9,11},{10,... | collective-permute-start | bytes 15368 | tf_op jit(solution)/shard_map/ppermute | solution.py:158
  41.7 0.8 %project_next.3.own_ref = f32[1,1280]{1,0:T(1,128)S(1)} custom-call(bf16[16,2048]{1,0:T(8,128)(2,1)S(1)} %get-tuple-element.7.left_ref, bf16[2048,5120]{1,0:T(8,128)(2,1)S(1)} %bitcast.9), custom_call_target="tpu_custom_call" | custom-call | flops 1000000000 | bytes 10000000 | tf_op jit(solution)/shard_map/project_next/pallas_call | solution.py:160
  42.5 0.0 collective-permute-done.1.b_ref
  42.5 1.1 %collective-permute-done.2.c_ref = f32[1,1280]{1,0:T(1,128)S(1)} collective-permute-done((f32[1,1280]{1,0:T(1,128)S(1)}, f32[1,1280]{1,0:T(1,128)S(1)}, u32[]{:S(2)}, u32[]{:S(2)}) %collective-permute-start.2) | collective-permute-done | bytes 5152 | tf_op jit(solution)/shard_map/ppermute | solution.py:158
  43.6 1.6 %collective-permute-done.a_ref = f32[1,1280]{1,0:T(1,128)S(1)} collective-permute-done((f32[1,1280]{1,0:T(1,128)S(1)}, f32[1,1280]{1,0:T(1,128)S(1)}, u32[]{:S(2)}, u32[]{:S(2)}) %collective-permute-start) | collective-permute-done | bytes 5152 | tf_op jit(solution)/shard_map/ppermute | solution.py:158
  45.3 0.6 %add_all.1 = bf16[1,1280]{1,0:T(2,128)(2,1)} custom-call(f32[1,1280]{1,0:T(1,128)S(1)} %project_next.3.own_ref, f32[1,1280]{1,0:T(1,128)S(1)} %collective-permute-done.a_ref, f32[1,1280]{1,0:T(1,128)S(1)} %collective-permute-done.1.b_ref, f32[1,1280]{1,0:T(1,128)S(1)} %collective-permute-done.2.c_ref), custom_call_target="tpu_custom_call" | custom-call | tf_op jit(solution)/shard_map/add_all/pallas_call | solution.py:169
  (2 shorter events, 0.0 us)
Async XLA Ops:
  0.0 34.0 %slice-start = ((s8[20971520]{0:T(1024)(128)(4,1)}), s8[4194304]{0:T(1024)(128)(4,1)S(1)}, s32[]{:S(2)}) async-start(s8[20971520]{0:T(1024)(128)(4,1)} %bitcast.4), calls=%async_computation.2 | async-start | bytes 8388608
  0.0 0.8 %copy-start.3 = (bf16[1,2,8,128]{3,2,1,0:T(8,128)(2,1)S(1)}, bf16[1,2,8,128]{3,2,1,0:T(8,128)(2,1)}, u32[]{:S(2)}) copy-start(bf16[1,2,8,128]{3,2,1,0:T(8,128)(2,1)} %param.5) | copy-start | bytes 12292
  0.8 16.2 %copy-start = (bf16[32,2,512,128]{3,2,1,0:T(8,128)(2,1)S(1)}, bf16[32,2,512,128]{3,2,1,0:T(8,128)(2,1)}, u32[]{:S(2)}) copy-start(bf16[32,2,512,128]{3,2,1,0:T(8,128)(2,1)} %key_ref.1) | copy-start | bytes 25165828
  0.8 16.2 %copy-start.1 = (bf16[32,2,512,128]{3,2,1,0:T(8,128)(2,1)S(1)}, bf16[32,2,512,128]{3,2,1,0:T(8,128)(2,1)}, u32[]{:S(2)}) copy-start(bf16[32,2,512,128]{3,2,1,0:T(8,128)(2,1)} %value_ref.1) | copy-start | bytes 25165828
  0.8 16.2 %copy-start.2 = (s32[32]{0:T(128)S(1)}, s32[32]{0:T(128)}, u32[]{:S(2)}) copy-start(s32[32]{0:T(128)} %used_ref.1) | copy-start | bytes 388
  0.8 33.2 %slice-start.1 = ((s8[20971520]{0:T(1024)(128)(4,1)}), s8[4194304]{0:T(1024)(128)(4,1)S(1)}, s32[]{:S(2)}) async-start(s8[20971520]{0:T(1024)(128)(4,1)} %bitcast.4), calls=%async_computation.3 | async-start | bytes 8388608
  0.9 33.2 %slice-start.2 = ((s8[20971520]{0:T(1024)(128)(4,1)}), s8[4194304]{0:T(1024)(128)(4,1)S(1)}, s32[]{:S(2)}) async-start(s8[20971520]{0:T(1024)(128)(4,1)} %bitcast.4), calls=%async_computation.4 | async-start | bytes 8388608
  0.9 33.2 %slice-start.3 = ((s8[20971520]{0:T(1024)(128)(4,1)}), s8[4194304]{0:T(1024)(128)(4,1)S(1)}, s32[]{:S(2)}) async-start(s8[20971520]{0:T(1024)(128)(4,1)} %bitcast.4), calls=%async_computation.5 | async-start | bytes 8388608
  0.9 33.2 %slice-start.4 = ((s8[20971520]{0:T(1024)(128)(4,1)}), s8[4194304]{0:T(1024)(128)(4,1)S(1)}, s32[]{:S(2)}) async-start(s8[20971520]{0:T(1024)(128)(4,1)} %bitcast.4), calls=%async_computation.6 | async-start | bytes 8388608
  36.9 5.6 %collective-permute-start.1 = (f32[1,1280]{1,0:T(1,128)S(1)}, f32[1,1280]{1,0:T(1,128)S(1)}, u32[]{:S(2)}, u32[]{:S(2)}) collective-permute-start(f32[1,1280]{1,0:T(1,128)S(1)} %project_next.4), channel_id=1, source_target_pairs={{0,3},{1,2},{2,1},{3,0},{4,7},{5,6},{6,5},{7,4},{8,11},{9,10},{10,... | collective-permute-start | bytes 15368 | tf_op jit(solution)/shard_map/ppermute | solution.py:158
  40.0 3.6 %collective-permute-start.2 = (f32[1,1280]{1,0:T(1,128)S(1)}, f32[1,1280]{1,0:T(1,128)S(1)}, u32[]{:S(2)}, u32[]{:S(2)}) collective-permute-start(f32[1,1280]{1,0:T(1,128)S(1)} %project_next.5), channel_id=1, source_target_pairs={{0,1},{1,0},{2,3},{3,2},{4,5},{5,4},{6,7},{7,6},{8,9},{9,8},{10,11... | collective-permute-start | bytes 15368 | tf_op jit(solution)/shard_map/ppermute | solution.py:158
  40.2 5.1 %collective-permute-start = (f32[1,1280]{1,0:T(1,128)S(1)}, f32[1,1280]{1,0:T(1,128)S(1)}, u32[]{:S(2)}, u32[]{:S(2)}) collective-permute-start(f32[1,1280]{1,0:T(1,128)S(1)} %get-tuple-element.8), channel_id=1, source_target_pairs={{0,2},{1,3},{2,0},{3,1},{4,6},{5,7},{6,4},{7,5},{8,10},{9,11},{10,... | collective-permute-start | bytes 15368 | tf_op jit(solution)/shard_map/ppermute | solution.py:158

commit v5 on v4

--- a/solution.py
+++ b/solution.py
@@ -9,9 +9,9 @@
 
 HEAD_SIZE = 128
 EMPTY = -1e30
-BLOCK = 8
+BLOCK = 32
 STEP = 256
-ORDER = (2, 3, 1, 0)
+NEAR, LAST = 1, 3
 TO_BASE_2 = HEAD_SIZE ** (-0.5) * 1.4426950408889634
 
 
@@ -104,8 +104,11 @@
     columns(left_ref[...], weight_ref, lax.axis_index("group") ^ away, out_ref)
 
 
-def add_all(own_ref, a_ref, b_ref, c_ref, out_ref):
-    total = (own_ref[...] + a_ref[...]) + (b_ref[...] + c_ref[...])
+def add_all(*refs):
+    out_ref = refs[-1]
+    total = refs[0][...]
+    for ref in refs[1:-1]:
+        total = total + ref[...]
     out_ref[...] = total.astype(out_ref.dtype)
 
 
@@ -145,19 +148,19 @@
     cost = pl.CostEstimate(flops=10**9, bytes_accessed=10**7, transcendentals=0)
     weight = vmem(out_weight.reshape(rows * HEAD_SIZE, width))
     left, term = pl.pallas_call(
-        functools.partial(project_first, ORDER[0]),
+        functools.partial(project_first, NEAR ^ LAST),
         out_shape=(jax.ShapeDtypeStruct((rows, rows * HEAD_SIZE), jnp.bfloat16), piece),
         in_specs=[whole, whole],
         out_specs=(whole, whole),
         compiler_params=small,
         name="project_first",
     )(vmem(arrived), weight)
-    pieces = []
-    for n, away in enumerate(ORDER[1:]):
-        pieces.append(
-            lax.ppermute(term, "group", [(j, j ^ ORDER[n]) for j in range(shares)])
-        )
-        term = pl.pallas_call(
+
+    def send(term, away):
+        return lax.ppermute(term, "group", [(j, j ^ away) for j in range(shares)])
+
+    def following(away):
+        return pl.pallas_call(
             functools.partial(project_next, away),
             out_shape=piece,
             in_specs=[whole, whole],
@@ -166,14 +169,22 @@
             compiler_params=small,
             name="project_next",
         )(left, weight)
-    return pl.pallas_call(
-        add_all,
-        out_shape=jax.ShapeDtypeStruct(piece.shape, jnp.bfloat16),
-        in_specs=[whole] * 4,
-        out_specs=whole,
-        compiler_params=small,
-        name="add_all",
-    )(term, *pieces)
+
+    def added(parts, dtype):
+        return pl.pallas_call(
+            add_all,
+            out_shape=jax.ShapeDtypeStruct(piece.shape, dtype),
+            in_specs=[whole] * len(parts),
+            out_specs=whole,
+            compiler_params=small,
+        )(*parts)
+
+    passed = send(term, NEAR)
+    direct = send(following(NEAR), NEAR)
+    beyond = following(LAST)
+    last = send(added([beyond, passed], jnp.float32), LAST)
+    own = following(0)
+    return added([own, direct, last], jnp.bfloat16)
 
 
 def solution(mesh):

time: 46.3 us -> 45 us (0.972)
  waiting for transfers between devices: 2.76 us -> 1.69 us
    ppermute x3, waiting for transfers between devices: 2.76 us -> 1.69 us  [send(): return lax.ppermute(term, 'group', [(j, j ^ away) for j in range(shares)])]
    pallas_call x5 -> x6, Pallas kernels: 4.23 us -> 4.22 us  [the longest x3 2.43 us: following(): pl.pallas_call(functools.partial(project_next, away), out_shape=piece, in...]
  transfers between devices with their start and end apart: 3 -> 3, of which waited for: 2 -> 2; matrix products, arithmetic and copies ran while one was open for 0% -> 0% of each run, Pallas kernels for 2% -> 4%
where the time goes in v5:
time: 45 us; the launch traced here: 44.9 us
  blocking collectives  28.5 us (63%)
  Pallas kernels  8.47 us (19%)
  starting transfers between devices  5.2 us (12%)
  waiting for transfers between devices  1.69 us (4%)
  local copies, waits for them, and re-layouts  0.87 us (2%)
    all_to_all x1, blocking collectives, per_device(): lax.all_to_all(copies, 'seq', split_axis=0, concat_axis=0, tiled=True)  16.1 us
    all_to_all x1, blocking collectives, per_device(): lax.all_to_all(packed.reshape(batch, rows + 1, 1, HEAD_SIZE), 'seq', spli...  12.4 us
    ppermute x3, starting transfers between devices, send(): return lax.ppermute(term, 'group', [(j, j ^ away) for j in range(shares)])  5.2 us
    pallas_call x1, Pallas kernels, per_device(): pl.pallas_call(attend, out_shape=jax.ShapeDtypeStruct((batch * (rows + 1)...  4.23 us
    pallas_call x3, Pallas kernels, following(): pl.pallas_call(functools.partial(project_next, away), out_shape=piece, in...  2.43 us
    ppermute x3, waiting for transfers between devices, send(): return lax.ppermute(term, 'group', [(j, j ^ away) for j in range(shares)])  1.69 us
    pallas_call x1, Pallas kernels, per_device(): pl.pallas_call(functools.partial(project_first, NEAR ^ LAST), out_shape=(...  1.18 us
  transfers between devices with their start and end apart: 3, of which 2 were waited for; matrix products, arithmetic and copies ran while one was open for 0% of the time, Pallas kernels for 4%

profile of v5, /device:TPU:0, one launch (start us, length us, event | category | flops | bytes accessed | tf_op | source)
XLA Modules:
  0.0 44.9 jit_solution(4239917661728606158)
XLA Ops:
  0.0 0.0 slice-start
  0.0 0.0 copy-start.3
  0.0 0.8 %copy-done.3 = bf16[1,2,8,128]{3,2,1,0:T(8,128)(2,1)S(1)} copy-done((bf16[1,2,8,128]{3,2,1,0:T(8,128)(2,1)S(1)}, bf16[1,2,8,128]{3,2,1,0:T(8,128)(2,1)}, u32[]{:S(2)}) %copy-start.3) | copy-done | bytes 4120
  0.8 0.0 copy-start
  0.8 0.0 copy-start.1
  0.8 0.0 copy-start.2
  0.8 0.0 slice-start.1
  0.9 0.0 slice-start.2
  0.9 0.0 slice-start.3
  0.9 0.0 slice-start.4
  0.9 16.1 %all_to_all.10.query_ref = bf16[32,16,128]{2,1,0:T(8,128)(2,1)S(1)} all-to-all(bf16[32,16,128]{2,1,0:T(8,128)(2,1)S(1)} %spread.1), channel_id=1, replica_groups=mesh['seq'=32,'group'=4] {'seq'}, dimensions={0} | all-to-all | bytes 262144 | tf_op jit(solution)/shard_map/all_to_all | solution.py:133
  17.0 0.0 copy-done
  17.0 0.0 copy-done.1
  17.0 0.0 copy-done.2
  17.0 4.2 %attend.1 = f32[544,128]{1,0:T(8,128)S(1)} custom-call(s32[32]{0:T(128)S(1)} %copy-done.2, bf16[32,16,128]{2,1,0:T(8,128)(2,1)S(1)} %all_to_all.10.query_ref, bf16[32,2,512,128]{3,2,1,0:T(8,128)(2,1)S(1)} %copy-done, bf16[32,2,512,128]{3,2,1,0:T(8,128)(2,1)S(1)} %copy-done.1), custom_call_target="tpu_custom_call" | custom-call | tf_op jit(solution)/shard_map/attend/pallas_call | solution.py:134
  21.3 12.4 %all_to_all.11 = f32[32,17,1,128]{3,2,1,0:T(1,128)S(1)} all-to-all(f32[32,17,1,128]{3,2,1,0:T(1,128)S(1)} %bitcast.11), channel_id=1, replica_groups=mesh['seq'=32,'group'=4] {'seq'}, dimensions={0} | all-to-all | bytes 557056 | tf_op jit(solution)/shard_map/all_to_all | solution.py:142
  33.7 0.0 slice-done
  33.7 0.0 slice-done.1
  33.7 0.0 slice-done.2
  33.7 0.0 slice-done.3
  33.7 0.0 slice-done.4
  33.7 1.2 %project_first.1 = (bf16[16,2048]{1,0:T(8,128)(2,1)S(1)}, f32[1,1280]{1,0:T(1,128)S(1)}) custom-call(f32[544,128]{1,0:T(8,128)S(1)} %bitcast.10, bf16[2048,5120]{1,0:T(8,128)(2,1)S(1)} %bitcast.6), custom_call_target="tpu_custom_call" | custom-call | tf_op jit(solution)/shard_map/project_first/pallas_call | solution.py:150
  34.9 0.8 %project_next.5.refs_0_ = f32[1,1280]{1,0:T(1,128)S(1)} custom-call(bf16[16,2048]{1,0:T(8,128)(2,1)S(1)} %get-tuple-element.7.left_ref, bf16[2048,5120]{1,0:T(8,128)(2,1)S(1)} %bitcast.7), custom_call_target="tpu_custom_call" | custom-call | flops 1000000000 | bytes 10000000 | tf_op jit(solution)/shard_map/project_next/pallas_call | solution.py:163
  35.7 1.7 %collective-permute-start.1 = (f32[1,1280]{1,0:T(1,128)S(1)}, f32[1,1280]{1,0:T(1,128)S(1)}, u32[]{:S(2)}, u32[]{:S(2)}) collective-permute-start(f32[1,1280]{1,0:T(1,128)S(1)} %get-tuple-element.8), channel_id=1, source_target_pairs={{0,1},{1,0},{2,3},{3,2},{4,5},{5,4},{6,7},{7,6},{8,9},{9,8},{10,11... | collective-permute-start | bytes 15368 | tf_op jit(solution)/shard_map/ppermute | solution.py:160
  37.4 0.8 %project_next.4 = f32[1,1280]{1,0:T(1,128)S(1)} custom-call(bf16[16,2048]{1,0:T(8,128)(2,1)S(1)} %get-tuple-element.7.left_ref, bf16[2048,5120]{1,0:T(8,128)(2,1)S(1)} %bitcast.8), custom_call_target="tpu_custom_call" | custom-call | flops 1000000000 | bytes 10000000 | tf_op jit(solution)/shard_map/project_next/pallas_call | solution.py:163
  38.2 0.5 %collective-permute-start = (f32[1,1280]{1,0:T(1,128)S(1)}, f32[1,1280]{1,0:T(1,128)S(1)}, u32[]{:S(2)}, u32[]{:S(2)}) collective-permute-start(f32[1,1280]{1,0:T(1,128)S(1)} %project_next.4), channel_id=1, source_target_pairs={{0,1},{1,0},{2,3},{3,2},{4,5},{5,4},{6,7},{7,6},{8,9},{9,8},{10,11... | collective-permute-start | bytes 15368 | tf_op jit(solution)/shard_map/ppermute | solution.py:160
  38.7 0.7 %collective-permute-done.1.refs_1_ = f32[1,1280]{1,0:T(1,128)S(1)} collective-permute-done((f32[1,1280]{1,0:T(1,128)S(1)}, f32[1,1280]{1,0:T(1,128)S(1)}, u32[]{:S(2)}, u32[]{:S(2)}) %collective-permute-start.1) | collective-permute-done | bytes 5152 | tf_op jit(solution)/shard_map/ppermute | solution.py:160
  39.4 3.0 %collective-permute-start.2 = (f32[1,1280]{1,0:T(1,128)S(1)}, f32[1,1280]{1,0:T(1,128)S(1)}, u32[]{:S(2)}, u32[]{:S(2)}) collective-permute-start(f32[1,1280]{1,0:T(1,128)S(1)} %shard_map.55), channel_id=1, source_target_pairs={{0,3},{1,2},{2,1},{3,0},{4,7},{5,6},{6,5},{7,4},{8,11},{9,10},{10,... | collective-permute-start | bytes 15368 | tf_op jit(solution)/shard_map/ppermute | solution.py:160
  42.5 0.8 %project_next.3.refs_0_ = f32[1,1280]{1,0:T(1,128)S(1)} custom-call(bf16[16,2048]{1,0:T(8,128)(2,1)S(1)} %get-tuple-element.7.left_ref, bf16[2048,5120]{1,0:T(8,128)(2,1)S(1)} %bitcast.9), custom_call_target="tpu_custom_call" | custom-call | flops 1000000000 | bytes 10000000 | tf_op jit(solution)/shard_map/project_next/pallas_call | solution.py:163
  43.3 0.0 collective-permute-done.refs_1_
  43.3 1.0 %collective-permute-done.2.refs_2_ = f32[1,1280]{1,0:T(1,128)S(1)} collective-permute-done((f32[1,1280]{1,0:T(1,128)S(1)}, f32[1,1280]{1,0:T(1,128)S(1)}, u32[]{:S(2)}, u32[]{:S(2)}) %collective-permute-start.2) | collective-permute-done | bytes 5152 | tf_op jit(solution)/shard_map/ppermute | solution.py:160
  44.3 0.6 %shard_map.56 = bf16[1,1280]{1,0:T(2,128)(2,1)} custom-call(f32[1,1280]{1,0:T(1,128)S(1)} %project_next.3.refs_0_, f32[1,1280]{1,0:T(1,128)S(1)} %collective-permute-done.refs_1_, f32[1,1280]{1,0:T(1,128)S(1)} %collective-permute-done.2.refs_2_), custom_call_target="tpu_custom_call" | custom-call | tf_op jit(solution)/shard_map/pallas_call | solution.py:174
  (3 shorter events, 0.0 us)
Async XLA Ops:
  0.0 33.7 %slice-start = ((s8[20971520]{0:T(1024)(128)(4,1)}), s8[4194304]{0:T(1024)(128)(4,1)S(1)}, s32[]{:S(2)}) async-start(s8[20971520]{0:T(1024)(128)(4,1)} %bitcast.4), calls=%async_computation.2 | async-start | bytes 8388608
  0.0 0.8 %copy-start.3 = (bf16[1,2,8,128]{3,2,1,0:T(8,128)(2,1)S(1)}, bf16[1,2,8,128]{3,2,1,0:T(8,128)(2,1)}, u32[]{:S(2)}) copy-start(bf16[1,2,8,128]{3,2,1,0:T(8,128)(2,1)} %param.5) | copy-start | bytes 12292
  0.8 16.2 %copy-start = (bf16[32,2,512,128]{3,2,1,0:T(8,128)(2,1)S(1)}, bf16[32,2,512,128]{3,2,1,0:T(8,128)(2,1)}, u32[]{:S(2)}) copy-start(bf16[32,2,512,128]{3,2,1,0:T(8,128)(2,1)} %key_ref.1) | copy-start | bytes 25165828
  0.8 16.2 %copy-start.1 = (bf16[32,2,512,128]{3,2,1,0:T(8,128)(2,1)S(1)}, bf16[32,2,512,128]{3,2,1,0:T(8,128)(2,1)}, u32[]{:S(2)}) copy-start(bf16[32,2,512,128]{3,2,1,0:T(8,128)(2,1)} %value_ref.1) | copy-start | bytes 25165828
  0.8 16.2 %copy-start.2 = (s32[32]{0:T(128)S(1)}, s32[32]{0:T(128)}, u32[]{:S(2)}) copy-start(s32[32]{0:T(128)} %used_ref.1) | copy-start | bytes 388
  0.8 32.8 %slice-start.1 = ((s8[20971520]{0:T(1024)(128)(4,1)}), s8[4194304]{0:T(1024)(128)(4,1)S(1)}, s32[]{:S(2)}) async-start(s8[20971520]{0:T(1024)(128)(4,1)} %bitcast.4), calls=%async_computation.3 | async-start | bytes 8388608
  0.9 32.8 %slice-start.2 = ((s8[20971520]{0:T(1024)(128)(4,1)}), s8[4194304]{0:T(1024)(128)(4,1)S(1)}, s32[]{:S(2)}) async-start(s8[20971520]{0:T(1024)(128)(4,1)} %bitcast.4), calls=%async_computation.4 | async-start | bytes 8388608
  0.9 32.8 %slice-start.3 = ((s8[20971520]{0:T(1024)(128)(4,1)}), s8[4194304]{0:T(1024)(128)(4,1)S(1)}, s32[]{:S(2)}) async-start(s8[20971520]{0:T(1024)(128)(4,1)} %bitcast.4), calls=%async_computation.5 | async-start | bytes 8388608
  0.9 32.8 %slice-start.4 = ((s8[20971520]{0:T(1024)(128)(4,1)}), s8[4194304]{0:T(1024)(128)(4,1)S(1)}, s32[]{:S(2)}) async-start(s8[20971520]{0:T(1024)(128)(4,1)} %bitcast.4), calls=%async_computation.6 | async-start | bytes 8388608
  35.7 3.7 %collective-permute-start.1 = (f32[1,1280]{1,0:T(1,128)S(1)}, f32[1,1280]{1,0:T(1,128)S(1)}, u32[]{:S(2)}, u32[]{:S(2)}) collective-permute-start(f32[1,1280]{1,0:T(1,128)S(1)} %get-tuple-element.8), channel_id=1, source_target_pairs={{0,1},{1,0},{2,3},{3,2},{4,5},{5,4},{6,7},{7,6},{8,9},{9,8},{10,11... | collective-permute-start | bytes 15368 | tf_op jit(solution)/shard_map/ppermute | solution.py:160
  38.2 5.1 %collective-permute-start = (f32[1,1280]{1,0:T(1,128)S(1)}, f32[1,1280]{1,0:T(1,128)S(1)}, u32[]{:S(2)}, u32[]{:S(2)}) collective-permute-start(f32[1,1280]{1,0:T(1,128)S(1)} %project_next.4), channel_id=1, source_target_pairs={{0,1},{1,0},{2,3},{3,2},{4,5},{5,4},{6,7},{7,6},{8,9},{9,8},{10,11... | collective-permute-start | bytes 15368 | tf_op jit(solution)/shard_map/ppermute | solution.py:160
  39.4 4.8 %collective-permute-start.2 = (f32[1,1280]{1,0:T(1,128)S(1)}, f32[1,1280]{1,0:T(1,128)S(1)}, u32[]{:S(2)}, u32[]{:S(2)}) collective-permute-start(f32[1,1280]{1,0:T(1,128)S(1)} %shard_map.55), channel_id=1, source_target_pairs={{0,3},{1,2},{2,1},{3,0},{4,7},{5,6},{6,5},{7,4},{8,11},{9,10},{10,... | collective-permute-start | bytes 15368 | tf_op jit(solution)/shard_map/ppermute | solution.py:160

commit v6 on v5

--- a/solution.py
+++ b/solution.py
@@ -9,7 +9,6 @@
 
 HEAD_SIZE = 128
 EMPTY = -1e30
-BLOCK = 32
 STEP = 256
 NEAR, LAST = 1, 3
 TO_BASE_2 = HEAD_SIZE ** (-0.5) * 1.4426950408889634
@@ -27,44 +26,41 @@
     def side_by_side(ref, b):
         return jnp.concatenate([ref[b, k] for k in range(heads)], axis=1)
 
-    def block(i, carry):
-        at = [i * BLOCK + j for j in range(BLOCK)]
-        logits = []
-        for b in at:
-            query = query_ref[b].astype(jnp.float32)
-            left = jnp.concatenate(
-                [jnp.where(row // group == k, query, 0.0) for k in range(heads)], axis=1
-            ).astype(jnp.bfloat16)
-            logits.append(
-                lax.dot_general(
-                    left, side_by_side(key_ref, b), (((1,), (1,)), ((), ())),
-                    preferred_element_type=jnp.float32,
-                )
-            )
-        filled = [place < used_ref[b] - first for b in at]
-        logits = [jnp.where(f, x * TO_BASE_2, EMPTY) for f, x in zip(filled, logits)]
-        tops = [jnp.max(x, axis=1, keepdims=True) for x in logits]
-        parts = [jnp.where(f, jnp.exp2(x - t), 0.0) for f, x, t in zip(filled, logits, tops)]
-        totals = [jnp.sum(p, axis=1, keepdims=True) for p in parts]
-        reads = []
-        for b, part in zip(at, parts):
-            high = part.astype(jnp.bfloat16)
-            low = (part - high.astype(jnp.float32)).astype(jnp.bfloat16)
-            both = jnp.dot(
-                jnp.concatenate([high, low], axis=0), side_by_side(value_ref, b),
+    used = used_ref[...] - first
+    at = range(batch)
+    logits = []
+    for b in at:
+        query = query_ref[b].astype(jnp.float32)
+        left = jnp.concatenate(
+            [jnp.where(row // group == k, query, 0.0) for k in range(heads)], axis=1
+        ).astype(jnp.bfloat16)
+        logits.append(
+            lax.dot_general(
+                left, side_by_side(key_ref, b), (((1,), (1,)), ((), ())),
                 preferred_element_type=jnp.float32,
             )
-            reads.append(both[:rows] + both[rows:])
-        for b, read, top, total in zip(at, reads, tops, totals):
-            for k in range(heads):
-                out_ref[pl.ds(b * (rows + 1) + k * group, group), :] = read[
-                    k * group : (k + 1) * group, k * HEAD_SIZE : (k + 1) * HEAD_SIZE
-                ]
-            stats = jnp.where(lane == row, top, jnp.where(lane == row + rows, total, 0.0))
-            out_ref[pl.ds(b * (rows + 1) + rows, 1), :] = jnp.sum(stats, axis=0, keepdims=True)
-        return carry
-
-    lax.fori_loop(0, batch // BLOCK, block, 0)
+        )
+    filled = [place < used[:, b : b + 1] for b in at]
+    logits = [jnp.where(f, x * TO_BASE_2, EMPTY) for f, x in zip(filled, logits)]
+    tops = [jnp.max(x, axis=1, keepdims=True) for x in logits]
+    parts = [jnp.where(f, jnp.exp2(x - t), 0.0) for f, x, t in zip(filled, logits, tops)]
+    totals = [jnp.sum(p, axis=1, keepdims=True) for p in parts]
+    reads = []
+    for b, part in zip(at, parts):
+        high = part.astype(jnp.bfloat16)
+        low = (part - high.astype(jnp.float32)).astype(jnp.bfloat16)
+        both = jnp.dot(
+            jnp.concatenate([high, low], axis=0), side_by_side(value_ref, b),
+            preferred_element_type=jnp.float32,
+        )
+        reads.append(both[:rows] + both[rows:])
+    for b, read, top, total in zip(at, reads, tops, totals):
+        for k in range(heads):
+            out_ref[pl.ds(b * (rows + 1) + k * group, group), :] = read[
+                k * group : (k + 1) * group, k * HEAD_SIZE : (k + 1) * HEAD_SIZE
+            ]
+        stats = jnp.where(lane == row, top, jnp.where(lane == row + rows, total, 0.0))
+        out_ref[pl.ds(b * (rows + 1) + rows, 1), :] = jnp.sum(stats, axis=0, keepdims=True)
 
 
 def spread(one_ref, out_ref):
@@ -73,13 +69,19 @@
 
 def merge(arrived_ref, rows):
     sources = arrived_ref.shape[0] // (rows + 1)
-    stats = jnp.transpose(arrived_ref[pl.ds(rows, sources, stride=rows + 1), :])
-    tops, sums = stats[:rows], stats[rows : 2 * rows]
-    scale = jnp.exp2(tops - jnp.max(tops, axis=1, keepdims=True))
-    scale = scale / jnp.sum(sums * scale, axis=1, keepdims=True)
-    read = jnp.zeros((rows, HEAD_SIZE), jnp.float32)
-    for s in range(sources):
-        read = read + arrived_ref[pl.ds(s * (rows + 1), rows), :] * scale[:, s : s + 1]
+    tops = arrived_ref[pl.ds(rows, sources, stride=rows + 1), :]
+    sums = pltpu.roll(tops, HEAD_SIZE - rows, 1)
+    scale = jnp.exp2(tops - jnp.max(tops, axis=0, keepdims=True))
+    total = jnp.sum(sums * scale, axis=0, keepdims=True)
+    lane = lax.broadcasted_iota(jnp.int32, total.shape, 1)
+    scale = scale / jnp.where(lane < rows, total, 1.0)
+    scale = jnp.transpose(scale)[:rows]
+    terms = [
+        arrived_ref[pl.ds(s * (rows + 1), rows), :] * scale[:, s : s + 1] for s in range(sources)
+    ]
+    while len(terms) > 1:
+        terms = [a + b for a, b in zip(terms[::2], terms[1::2])]
+    read = terms[0]
     row = lax.broadcasted_iota(jnp.int32, (rows, HEAD_SIZE), 0)
     return jnp.concatenate(
         [jnp.where(row == r, read, 0.0).astype(jnp.bfloat16) for r in range(rows)], axis=1
@@ -134,11 +136,11 @@
     packed = pl.pallas_call(
         attend,
         out_shape=jax.ShapeDtypeStruct((batch * (rows + 1), HEAD_SIZE), jnp.float32),
-        in_specs=[pl.BlockSpec(memory_space=pltpu.SMEM), whole, whole, whole],
+        in_specs=[whole] * 4,
         out_specs=whole,
         compiler_params=pltpu.CompilerParams(vmem_limit_bytes=8 << 20),
         name="attend",
-    )(used_length, vmem(all_queries), vmem(stored_keys), vmem(stored_values))
+    )(used_length.reshape(1, batch), vmem(all_queries), vmem(stored_keys), vmem(stored_values))
     arrived = lax.all_to_all(
         packed.reshape(batch, rows + 1, 1, HEAD_SIZE), "seq", split_axis=0, concat_axis=0, tiled=True
     ).reshape(packed.shape)

time: 45 us -> 44.6 us (level)
  Pallas kernels: 8.47 us -> 8.02 us
where the time goes in v6:
time: 44.6 us; the launch traced here: 44.4 us
  blocking collectives  28.5 us (64%)
  Pallas kernels  8.02 us (18%)
  starting transfers between devices  5.19 us (12%)
  waiting for transfers between devices  1.7 us (4%)
  local copies, waits for them, and re-layouts  0.87 us (2%)
    all_to_all x1, blocking collectives, per_device(): lax.all_to_all(copies, 'seq', split_axis=0, concat_axis=0, tiled=True)  16.1 us
    all_to_all x1, blocking collectives, per_device(): lax.all_to_all(packed.reshape(batch, rows + 1, 1, HEAD_SIZE), 'seq', spli...  12.4 us
    ppermute x3, starting transfers between devices, send(): return lax.ppermute(term, 'group', [(j, j ^ away) for j in range(shares)])  5.19 us
    pallas_call x1, Pallas kernels, per_device(): pl.pallas_call(attend, out_shape=jax.ShapeDtypeStruct((batch * (rows + 1)...  3.84 us
    pallas_call x3, Pallas kernels, following(): pl.pallas_call(functools.partial(project_next, away), out_shape=piece, in...  2.43 us
    ppermute x3, waiting for transfers between devices, send(): return lax.ppermute(term, 'group', [(j, j ^ away) for j in range(shares)])  1.7 us
    pallas_call x1, Pallas kernels, per_device(): pl.pallas_call(functools.partial(project_first, NEAR ^ LAST), out_shape=(...  1.12 us
  transfers between devices with their start and end apart: 3, of which 2 were waited for; matrix products, arithmetic and copies ran while one was open for 0% of the time, Pallas kernels for 4%

profile of v6, /device:TPU:0, one launch (start us, length us, event | category | flops | bytes accessed | tf_op | source)
XLA Modules:
  0.0 44.4 jit_solution(628917478076914990)
XLA Ops:
  0.0 0.0 slice-start
  0.0 0.0 copy-start.3
  0.0 0.8 %copy-done.3 = bf16[1,2,8,128]{3,2,1,0:T(8,128)(2,1)S(1)} copy-done((bf16[1,2,8,128]{3,2,1,0:T(8,128)(2,1)S(1)}, bf16[1,2,8,128]{3,2,1,0:T(8,128)(2,1)}, u32[]{:S(2)}) %copy-start.3) | copy-done | bytes 4120
  0.8 0.0 copy-start
  0.8 0.0 copy-start.1
  0.8 0.0 copy-start.2
  0.8 0.0 slice-start.1
  0.9 0.0 slice-start.2
  0.9 0.0 slice-start.3
  0.9 0.0 slice-start.4
  0.9 16.1 %all_to_all.10.query_ref = bf16[32,16,128]{2,1,0:T(8,128)(2,1)S(1)} all-to-all(bf16[32,16,128]{2,1,0:T(8,128)(2,1)S(1)} %spread.1), channel_id=1, replica_groups=mesh['seq'=32,'group'=4] {'seq'}, dimensions={0} | all-to-all | bytes 262144 | tf_op jit(solution)/shard_map/all_to_all | solution.py:135
  17.0 0.0 copy-done
  17.0 0.0 copy-done.1
  17.0 0.0 copy-done.2
  17.0 3.8 %attend.1 = f32[544,128]{1,0:T(8,128)S(1)} custom-call(s32[1,32]{1,0:T(1,128)S(1)} %bitcast.13, bf16[32,16,128]{2,1,0:T(8,128)(2,1)S(1)} %all_to_all.10.query_ref, bf16[32,2,512,128]{3,2,1,0:T(8,128)(2,1)S(1)} %copy-done, bf16[32,2,512,128]{3,2,1,0:T(8,128)(2,1)S(1)} %copy-done.1), custom_call_target="tpu_custom_call" | custom-call | tf_op jit(solution)/shard_map/attend/pallas_call | solution.py:136
  20.9 12.4 %all_to_all.11 = f32[32,17,1,128]{3,2,1,0:T(1,128)S(1)} all-to-all(f32[32,17,1,128]{3,2,1,0:T(1,128)S(1)} %bitcast.12), channel_id=1, replica_groups=mesh['seq'=32,'group'=4] {'seq'}, dimensions={0} | all-to-all | bytes 557056 | tf_op jit(solution)/shard_map/all_to_all | solution.py:144
  33.3 0.0 slice-done
  33.3 0.0 slice-done.1
  33.3 0.0 slice-done.2
  33.3 0.0 slice-done.3
  33.3 0.0 slice-done.4
  33.3 1.1 %project_first.1 = (bf16[16,2048]{1,0:T(8,128)(2,1)S(1)}, f32[1,1280]{1,0:T(1,128)S(1)}) custom-call(f32[544,128]{1,0:T(8,128)S(1)} %bitcast.11, bf16[2048,5120]{1,0:T(8,128)(2,1)S(1)} %bitcast.7), custom_call_target="tpu_custom_call" | custom-call | tf_op jit(solution)/shard_map/project_first/pallas_call | solution.py:152
  34.5 0.8 %project_next.5.refs_0_ = f32[1,1280]{1,0:T(1,128)S(1)} custom-call(bf16[16,2048]{1,0:T(8,128)(2,1)S(1)} %get-tuple-element.7.left_ref, bf16[2048,5120]{1,0:T(8,128)(2,1)S(1)} %bitcast.8), custom_call_target="tpu_custom_call" | custom-call | flops 1000000000 | bytes 10000000 | tf_op jit(solution)/shard_map/project_next/pallas_call | solution.py:165
  35.3 1.7 %collective-permute-start.1 = (f32[1,1280]{1,0:T(1,128)S(1)}, f32[1,1280]{1,0:T(1,128)S(1)}, u32[]{:S(2)}, u32[]{:S(2)}) collective-permute-start(f32[1,1280]{1,0:T(1,128)S(1)} %get-tuple-element.8), channel_id=1, source_target_pairs={{0,1},{1,0},{2,3},{3,2},{4,5},{5,4},{6,7},{7,6},{8,9},{9,8},{10,11... | collective-permute-start | bytes 15368 | tf_op jit(solution)/shard_map/ppermute | solution.py:162
  37.0 0.8 %project_next.4 = f32[1,1280]{1,0:T(1,128)S(1)} custom-call(bf16[16,2048]{1,0:T(8,128)(2,1)S(1)} %get-tuple-element.7.left_ref, bf16[2048,5120]{1,0:T(8,128)(2,1)S(1)} %bitcast.9), custom_call_target="tpu_custom_call" | custom-call | flops 1000000000 | bytes 10000000 | tf_op jit(solution)/shard_map/project_next/pallas_call | solution.py:165
  37.8 0.5 %collective-permute-start = (f32[1,1280]{1,0:T(1,128)S(1)}, f32[1,1280]{1,0:T(1,128)S(1)}, u32[]{:S(2)}, u32[]{:S(2)}) collective-permute-start(f32[1,1280]{1,0:T(1,128)S(1)} %project_next.4), channel_id=1, source_target_pairs={{0,1},{1,0},{2,3},{3,2},{4,5},{5,4},{6,7},{7,6},{8,9},{9,8},{10,11... | collective-permute-start | bytes 15368 | tf_op jit(solution)/shard_map/ppermute | solution.py:162
  38.3 0.7 %collective-permute-done.1.refs_1_ = f32[1,1280]{1,0:T(1,128)S(1)} collective-permute-done((f32[1,1280]{1,0:T(1,128)S(1)}, f32[1,1280]{1,0:T(1,128)S(1)}, u32[]{:S(2)}, u32[]{:S(2)}) %collective-permute-start.1) | collective-permute-done | bytes 5152 | tf_op jit(solution)/shard_map/ppermute | solution.py:162
  39.0 3.0 %collective-permute-start.2 = (f32[1,1280]{1,0:T(1,128)S(1)}, f32[1,1280]{1,0:T(1,128)S(1)}, u32[]{:S(2)}, u32[]{:S(2)}) collective-permute-start(f32[1,1280]{1,0:T(1,128)S(1)} %shard_map.55), channel_id=1, source_target_pairs={{0,3},{1,2},{2,1},{3,0},{4,7},{5,6},{6,5},{7,4},{8,11},{9,10},{10,... | collective-permute-start | bytes 15368 | tf_op jit(solution)/shard_map/ppermute | solution.py:162
  42.0 0.8 %project_next.3.refs_0_ = f32[1,1280]{1,0:T(1,128)S(1)} custom-call(bf16[16,2048]{1,0:T(8,128)(2,1)S(1)} %get-tuple-element.7.left_ref, bf16[2048,5120]{1,0:T(8,128)(2,1)S(1)} %bitcast.10), custom_call_target="tpu_custom_call" | custom-call | flops 1000000000 | bytes 10000000 | tf_op jit(solution)/shard_map/project_next/pallas_call | solution.py:165
  42.8 0.0 collective-permute-done.refs_1_
  42.8 1.0 %collective-permute-done.2.refs_2_ = f32[1,1280]{1,0:T(1,128)S(1)} collective-permute-done((f32[1,1280]{1,0:T(1,128)S(1)}, f32[1,1280]{1,0:T(1,128)S(1)}, u32[]{:S(2)}, u32[]{:S(2)}) %collective-permute-start.2) | collective-permute-done | bytes 5152 | tf_op jit(solution)/shard_map/ppermute | solution.py:162
  43.8 0.6 %shard_map.56 = bf16[1,1280]{1,0:T(2,128)(2,1)} custom-call(f32[1,1280]{1,0:T(1,128)S(1)} %project_next.3.refs_0_, f32[1,1280]{1,0:T(1,128)S(1)} %collective-permute-done.refs_1_, f32[1,1280]{1,0:T(1,128)S(1)} %collective-permute-done.2.refs_2_), custom_call_target="tpu_custom_call" | custom-call | tf_op jit(solution)/shard_map/pallas_call | solution.py:176
  (3 shorter events, 0.0 us)
Async XLA Ops:
  0.0 33.3 %slice-start = ((s8[20971520]{0:T(1024)(128)(4,1)}), s8[4194304]{0:T(1024)(128)(4,1)S(1)}, s32[]{:S(2)}) async-start(s8[20971520]{0:T(1024)(128)(4,1)} %bitcast.5), calls=%async_computation.2 | async-start | bytes 8388608
  0.0 0.8 %copy-start.3 = (bf16[1,2,8,128]{3,2,1,0:T(8,128)(2,1)S(1)}, bf16[1,2,8,128]{3,2,1,0:T(8,128)(2,1)}, u32[]{:S(2)}) copy-start(bf16[1,2,8,128]{3,2,1,0:T(8,128)(2,1)} %param.5) | copy-start | bytes 12292
  0.8 16.2 %copy-start = (bf16[32,2,512,128]{3,2,1,0:T(8,128)(2,1)S(1)}, bf16[32,2,512,128]{3,2,1,0:T(8,128)(2,1)}, u32[]{:S(2)}) copy-start(bf16[32,2,512,128]{3,2,1,0:T(8,128)(2,1)} %key_ref.1) | copy-start | bytes 25165828
  0.8 16.2 %copy-start.1 = (bf16[32,2,512,128]{3,2,1,0:T(8,128)(2,1)S(1)}, bf16[32,2,512,128]{3,2,1,0:T(8,128)(2,1)}, u32[]{:S(2)}) copy-start(bf16[32,2,512,128]{3,2,1,0:T(8,128)(2,1)} %value_ref.1) | copy-start | bytes 25165828
  0.8 16.2 %copy-start.2 = (s32[32]{0:T(128)S(1)}, s32[32]{0:T(128)}, u32[]{:S(2)}) copy-start(s32[32]{0:T(128)} %param.8) | copy-start | bytes 388
  0.8 32.5 %slice-start.1 = ((s8[20971520]{0:T(1024)(128)(4,1)}), s8[4194304]{0:T(1024)(128)(4,1)S(1)}, s32[]{:S(2)}) async-start(s8[20971520]{0:T(1024)(128)(4,1)} %bitcast.5), calls=%async_computation.3 | async-start | bytes 8388608
  0.9 32.5 %slice-start.2 = ((s8[20971520]{0:T(1024)(128)(4,1)}), s8[4194304]{0:T(1024)(128)(4,1)S(1)}, s32[]{:S(2)}) async-start(s8[20971520]{0:T(1024)(128)(4,1)} %bitcast.5), calls=%async_computation.4 | async-start | bytes 8388608
  0.9 32.5 %slice-start.3 = ((s8[20971520]{0:T(1024)(128)(4,1)}), s8[4194304]{0:T(1024)(128)(4,1)S(1)}, s32[]{:S(2)}) async-start(s8[20971520]{0:T(1024)(128)(4,1)} %bitcast.5), calls=%async_computation.5 | async-start | bytes 8388608
  0.9 32.5 %slice-start.4 = ((s8[20971520]{0:T(1024)(128)(4,1)}), s8[4194304]{0:T(1024)(128)(4,1)S(1)}, s32[]{:S(2)}) async-start(s8[20971520]{0:T(1024)(128)(4,1)} %bitcast.5), calls=%async_computation.6 | async-start | bytes 8388608
  35.3 3.7 %collective-permute-start.1 = (f32[1,1280]{1,0:T(1,128)S(1)}, f32[1,1280]{1,0:T(1,128)S(1)}, u32[]{:S(2)}, u32[]{:S(2)}) collective-permute-start(f32[1,1280]{1,0:T(1,128)S(1)} %get-tuple-element.8), channel_id=1, source_target_pairs={{0,1},{1,0},{2,3},{3,2},{4,5},{5,4},{6,7},{7,6},{8,9},{9,8},{10,11... | collective-permute-start | bytes 15368 | tf_op jit(solution)/shard_map/ppermute | solution.py:162
  37.8 5.1 %collective-permute-start = (f32[1,1280]{1,0:T(1,128)S(1)}, f32[1,1280]{1,0:T(1,128)S(1)}, u32[]{:S(2)}, u32[]{:S(2)}) collective-permute-start(f32[1,1280]{1,0:T(1,128)S(1)} %project_next.4), channel_id=1, source_target_pairs={{0,1},{1,0},{2,3},{3,2},{4,5},{5,4},{6,7},{7,6},{8,9},{9,8},{10,11... | collective-permute-start | bytes 15368 | tf_op jit(solution)/shard_map/ppermute | solution.py:162
  39.0 4.8 %collective-permute-start.2 = (f32[1,1280]{1,0:T(1,128)S(1)}, f32[1,1280]{1,0:T(1,128)S(1)}, u32[]{:S(2)}, u32[]{:S(2)}) collective-permute-start(f32[1,1280]{1,0:T(1,128)S(1)} %shard_map.55), channel_id=1, source_target_pairs={{0,3},{1,2},{2,1},{3,0},{4,7},{5,6},{6,5},{7,4},{8,11},{9,10},{10,... | collective-permute-start | bytes 15368 | tf_op jit(solution)/shard_map/ppermute | solution.py:162

commit v7 on v6

--- a/solution.py
+++ b/solution.py
@@ -8,10 +8,25 @@
 from jax.sharding import PartitionSpec as P
 
 HEAD_SIZE = 128
-EMPTY = -1e30
+EMPTY = -4000.0
+TINY = 1e-30
+SPAN = 16384.0
+LOG2_E = 1.4426950408889634
 STEP = 256
 NEAR, LAST = 1, 3
-TO_BASE_2 = HEAD_SIZE ** (-0.5) * 1.4426950408889634
+TO_BASE_2 = HEAD_SIZE ** (-0.5) * LOG2_E
+
+
+def log2(x):
+    return jnp.log(x) * LOG2_E
+
+
+def split(x):
+    first = jnp.floor(x * 0.25 + 0.5)
+    x = x - first * 4.0
+    second = jnp.floor(x * 2.0**9 + 0.5)
+    x = x - second * 2.0**-9
+    return first, second, jnp.floor(x * 2.0**20 + 0.5)
 
 
 def attend(used_ref, query_ref, key_ref, value_ref, out_ref):
@@ -55,12 +70,22 @@
         )
         reads.append(both[:rows] + both[rows:])
     for b, read, top, total in zip(at, reads, tops, totals):
-        for k in range(heads):
-            out_ref[pl.ds(b * (rows + 1) + k * group, group), :] = read[
-                k * group : (k + 1) * group, k * HEAD_SIZE : (k + 1) * HEAD_SIZE
-            ]
-        stats = jnp.where(lane == row, top, jnp.where(lane == row + rows, total, 0.0))
-        out_ref[pl.ds(b * (rows + 1) + rows, 1), :] = jnp.sum(stats, axis=0, keepdims=True)
+        read = jnp.concatenate(
+            [
+                read[k * group : (k + 1) * group, k * HEAD_SIZE : (k + 1) * HEAD_SIZE]
+                for k in range(heads)
+            ],
+            axis=0,
+        )
+        largest = jnp.maximum(jnp.max(jnp.abs(read), axis=1, keepdims=True), TINY)
+        out_ref[pl.ds(b * (rows + 2), rows), :] = read * (SPAN / largest)
+        pieces = split(top + log2(largest / SPAN)) + split(top + log2(jnp.maximum(total, TINY)))
+        stats = jnp.zeros((rows, HEAD_SIZE), jnp.float32)
+        for i, piece in enumerate(pieces):
+            stats = jnp.where(lane == row + i * rows, piece, stats)
+        out_ref[pl.ds(b * (rows + 2) + rows, 2), :] = jnp.broadcast_to(
+            jnp.sum(stats, axis=0, keepdims=True), (2, HEAD_SIZE)
+        )
 
 
 def spread(one_ref, out_ref):
@@ -68,16 +93,21 @@
 
 
 def merge(arrived_ref, rows):
-    sources = arrived_ref.shape[0] // (rows + 1)
-    tops = arrived_ref[pl.ds(rows, sources, stride=rows + 1), :]
-    sums = pltpu.roll(tops, HEAD_SIZE - rows, 1)
-    scale = jnp.exp2(tops - jnp.max(tops, axis=0, keepdims=True))
-    total = jnp.sum(sums * scale, axis=0, keepdims=True)
-    lane = lax.broadcasted_iota(jnp.int32, total.shape, 1)
-    scale = scale / jnp.where(lane < rows, total, 1.0)
+    sources = arrived_ref.shape[0] // (rows + 2)
+    stats = arrived_ref[pl.ds(rows, sources, stride=rows + 2), :]
+    stats = (
+        stats * 4.0
+        + pltpu.roll(stats, HEAD_SIZE - rows, 1) * 2.0**-9
+        + pltpu.roll(stats, HEAD_SIZE - 2 * rows, 1) * 2.0**-20
+    )
+    mine = lax.broadcasted_iota(jnp.int32, stats.shape, 1) < rows
+    sums = jnp.where(mine, pltpu.roll(stats, HEAD_SIZE - 3 * rows, 1), 0.0)
+    tops = jnp.where(mine, stats, 0.0)
+    most = jnp.max(sums, axis=0, keepdims=True)
+    scale = jnp.exp2(tops - most) / jnp.sum(jnp.exp2(sums - most), axis=0, keepdims=True)
     scale = jnp.transpose(scale)[:rows]
     terms = [
-        arrived_ref[pl.ds(s * (rows + 1), rows), :] * scale[:, s : s + 1] for s in range(sources)
+        arrived_ref[pl.ds(s * (rows + 2), rows), :] * scale[:, s : s + 1] for s in range(sources)
     ]
     while len(terms) > 1:
         terms = [a + b for a, b in zip(terms[::2], terms[1::2])]
@@ -135,15 +165,15 @@
     all_queries = lax.all_to_all(copies, "seq", split_axis=0, concat_axis=0, tiled=True)
     packed = pl.pallas_call(
         attend,
-        out_shape=jax.ShapeDtypeStruct((batch * (rows + 1), HEAD_SIZE), jnp.float32),
+        out_shape=jax.ShapeDtypeStruct((batch * (rows + 2), HEAD_SIZE), jnp.float32),
         in_specs=[whole] * 4,
         out_specs=whole,
         compiler_params=pltpu.CompilerParams(vmem_limit_bytes=8 << 20),
         name="attend",
     )(used_length.reshape(1, batch), vmem(all_queries), vmem(stored_keys), vmem(stored_values))
-    arrived = lax.all_to_all(
-        packed.reshape(batch, rows + 1, 1, HEAD_SIZE), "seq", split_axis=0, concat_axis=0, tiled=True
-    ).reshape(packed.shape)
+    halves = packed.astype(jnp.float16).reshape(batch, (rows + 2) // 2, 2, HEAD_SIZE)
+    halves = lax.all_to_all(halves, "seq", split_axis=0, concat_axis=0, tiled=True)
+    arrived = halves.reshape(packed.shape).astype(jnp.float32)
     shares = lax.axis_size("group")
     piece = jax.ShapeDtypeStruct((1, width // shares), jnp.float32)
     small = pltpu.CompilerParams(vmem_limit_bytes=8 << 20)

time: 44.6 us -> 43.8 us (0.982)
  blocking collectives: 28.5 us -> 27.5 us
    all_to_all x1, blocking collectives: 12.4 us -> 11.4 us  [per_device(): lax.all_to_all(halves, 'seq', split_axis=0, concat_axis=0, tiled=True)]
where the time goes in v7:
time: 43.8 us; the launch traced here: 43.7 us
  blocking collectives  27.5 us (63%)
  Pallas kernels  8.23 us (19%)
  starting transfers between devices  5.2 us (12%)
  waiting for transfers between devices  1.7 us (4%)
  local copies, waits for them, and re-layouts  0.87 us (2%)
    all_to_all x1, blocking collectives, per_device(): lax.all_to_all(copies, 'seq', split_axis=0, concat_axis=0, tiled=True)  16.1 us
    all_to_all x1, blocking collectives, per_device(): lax.all_to_all(halves, 'seq', split_axis=0, concat_axis=0, tiled=True)  11.4 us
    ppermute x3, starting transfers between devices, send(): return lax.ppermute(term, 'group', [(j, j ^ away) for j in range(shares)])  5.2 us
    pallas_call x1, Pallas kernels, per_device(): pl.pallas_call(attend, out_shape=jax.ShapeDtypeStruct((batch * (rows + 2)...  3.95 us
    pallas_call x3, Pallas kernels, following(): pl.pallas_call(functools.partial(project_next, away), out_shape=piece, in...  2.43 us
    ppermute x3, waiting for transfers between devices, send(): return lax.ppermute(term, 'group', [(j, j ^ away) for j in range(shares)])  1.7 us
    pallas_call x1, Pallas kernels, per_device(): pl.pallas_call(functools.partial(project_first, NEAR ^ LAST), out_shape=(...  1.21 us
  transfers between devices with their start and end apart: 3, of which 2 were waited for; matrix products, arithmetic and copies ran while one was open for 0% of the time, Pallas kernels for 4%

profile of v7, /device:TPU:0, one launch (start us, length us, event | category | flops | bytes accessed | tf_op | source)
XLA Modules:
  0.0 43.7 jit_solution(3777092770671819949)
XLA Ops:
  0.0 0.0 slice-start
  0.0 0.0 copy-start.3
  0.0 0.8 %copy-done.3 = bf16[1,2,8,128]{3,2,1,0:T(8,128)(2,1)S(1)} copy-done((bf16[1,2,8,128]{3,2,1,0:T(8,128)(2,1)S(1)}, bf16[1,2,8,128]{3,2,1,0:T(8,128)(2,1)}, u32[]{:S(2)}) %copy-start.3) | copy-done | bytes 4120
  0.8 0.0 copy-start
  0.8 0.0 copy-start.1
  0.8 0.0 copy-start.2
  0.8 0.0 slice-start.1
  0.9 0.0 slice-start.2
  0.9 0.0 slice-start.3
  0.9 0.0 slice-start.4
  0.9 16.1 %all_to_all.10.query_ref = bf16[32,16,128]{2,1,0:T(8,128)(2,1)S(1)} all-to-all(bf16[32,16,128]{2,1,0:T(8,128)(2,1)S(1)} %spread.1), channel_id=1, replica_groups=mesh['seq'=32,'group'=4] {'seq'}, dimensions={0} | all-to-all | bytes 262144 | tf_op jit(solution)/shard_map/all_to_all | solution.py:165
  17.0 0.0 copy-done
  17.0 0.0 copy-done.1
  17.0 0.0 copy-done.2
  17.0 4.0 %attend.1 = f32[576,128]{1,0:T(8,128)S(1)} custom-call(s32[1,32]{1,0:T(1,128)S(1)} %bitcast.12, bf16[32,16,128]{2,1,0:T(8,128)(2,1)S(1)} %all_to_all.10.query_ref, bf16[32,2,512,128]{3,2,1,0:T(8,128)(2,1)S(1)} %copy-done, bf16[32,2,512,128]{3,2,1,0:T(8,128)(2,1)S(1)} %copy-done.1), custom_call_target="tpu_custom_call" | custom-call | tf_op jit(solution)/shard_map/attend/pallas_call | solution.py:166
  21.0 11.4 %all_to_all.11 = f16[32,9,2,128]{3,2,1,0:T(2,128)(2,1)S(1)} all-to-all(f16[32,9,2,128]{3,2,1,0:T(2,128)(2,1)S(1)} %bitcast.14), channel_id=1, replica_groups=mesh['seq'=32,'group'=4] {'seq'}, dimensions={0} | all-to-all | bytes 294912 | tf_op jit(solution)/shard_map/all_to_all | solution.py:175
  32.4 0.0 slice-done
  32.4 0.0 slice-done.1
  32.4 0.0 slice-done.2
  32.5 0.0 slice-done.3
  32.5 0.0 slice-done.4
  32.5 1.2 %project_first.1 = (bf16[16,2048]{1,0:T(8,128)(2,1)S(1)}, f32[1,1280]{1,0:T(1,128)S(1)}) custom-call(f32[576,128]{1,0:T(8,128)S(1)} %convert.1.arrived_ref, bf16[2048,5120]{1,0:T(8,128)(2,1)S(1)} %bitcast.8), custom_call_target="tpu_custom_call" | custom-call | tf_op jit(solution)/shard_map/project_first/pallas_call | solution.py:182
  33.7 0.8 %project_next.5.refs_0_ = f32[1,1280]{1,0:T(1,128)S(1)} custom-call(bf16[16,2048]{1,0:T(8,128)(2,1)S(1)} %get-tuple-element.7.left_ref, bf16[2048,5120]{1,0:T(8,128)(2,1)S(1)} %bitcast.9), custom_call_target="tpu_custom_call" | custom-call | flops 1000000000 | bytes 10000000 | tf_op jit(solution)/shard_map/project_next/pallas_call | solution.py:195
  34.5 1.7 %collective-permute-start.1 = (f32[1,1280]{1,0:T(1,128)S(1)}, f32[1,1280]{1,0:T(1,128)S(1)}, u32[]{:S(2)}, u32[]{:S(2)}) collective-permute-start(f32[1,1280]{1,0:T(1,128)S(1)} %get-tuple-element.8), channel_id=1, source_target_pairs={{0,1},{1,0},{2,3},{3,2},{4,5},{5,4},{6,7},{7,6},{8,9},{9,8},{10,11... | collective-permute-start | bytes 15368 | tf_op jit(solution)/shard_map/ppermute | solution.py:192
  36.2 0.8 %project_next.4 = f32[1,1280]{1,0:T(1,128)S(1)} custom-call(bf16[16,2048]{1,0:T(8,128)(2,1)S(1)} %get-tuple-element.7.left_ref, bf16[2048,5120]{1,0:T(8,128)(2,1)S(1)} %bitcast.10), custom_call_target="tpu_custom_call" | custom-call | flops 1000000000 | bytes 10000000 | tf_op jit(solution)/shard_map/project_next/pallas_call | solution.py:195
  37.0 0.5 %collective-permute-start = (f32[1,1280]{1,0:T(1,128)S(1)}, f32[1,1280]{1,0:T(1,128)S(1)}, u32[]{:S(2)}, u32[]{:S(2)}) collective-permute-start(f32[1,1280]{1,0:T(1,128)S(1)} %project_next.4), channel_id=1, source_target_pairs={{0,1},{1,0},{2,3},{3,2},{4,5},{5,4},{6,7},{7,6},{8,9},{9,8},{10,11... | collective-permute-start | bytes 15368 | tf_op jit(solution)/shard_map/ppermute | solution.py:192
  37.5 0.7 %collective-permute-done.1.refs_1_ = f32[1,1280]{1,0:T(1,128)S(1)} collective-permute-done((f32[1,1280]{1,0:T(1,128)S(1)}, f32[1,1280]{1,0:T(1,128)S(1)}, u32[]{:S(2)}, u32[]{:S(2)}) %collective-permute-start.1) | collective-permute-done | bytes 5152 | tf_op jit(solution)/shard_map/ppermute | solution.py:192
  38.2 3.0 %collective-permute-start.2 = (f32[1,1280]{1,0:T(1,128)S(1)}, f32[1,1280]{1,0:T(1,128)S(1)}, u32[]{:S(2)}, u32[]{:S(2)}) collective-permute-start(f32[1,1280]{1,0:T(1,128)S(1)} %shard_map.55), channel_id=1, source_target_pairs={{0,3},{1,2},{2,1},{3,0},{4,7},{5,6},{6,5},{7,4},{8,11},{9,10},{10,... | collective-permute-start | bytes 15368 | tf_op jit(solution)/shard_map/ppermute | solution.py:192
  41.2 0.8 %project_next.3.refs_0_ = f32[1,1280]{1,0:T(1,128)S(1)} custom-call(bf16[16,2048]{1,0:T(8,128)(2,1)S(1)} %get-tuple-element.7.left_ref, bf16[2048,5120]{1,0:T(8,128)(2,1)S(1)} %bitcast.11), custom_call_target="tpu_custom_call" | custom-call | flops 1000000000 | bytes 10000000 | tf_op jit(solution)/shard_map/project_next/pallas_call | solution.py:195
  42.1 0.0 collective-permute-done.refs_1_
  42.1 1.0 %collective-permute-done.2.refs_2_ = f32[1,1280]{1,0:T(1,128)S(1)} collective-permute-done((f32[1,1280]{1,0:T(1,128)S(1)}, f32[1,1280]{1,0:T(1,128)S(1)}, u32[]{:S(2)}, u32[]{:S(2)}) %collective-permute-start.2) | collective-permute-done | bytes 5152 | tf_op jit(solution)/shard_map/ppermute | solution.py:192
  43.1 0.6 %shard_map.56 = bf16[1,1280]{1,0:T(2,128)(2,1)} custom-call(f32[1,1280]{1,0:T(1,128)S(1)} %project_next.3.refs_0_, f32[1,1280]{1,0:T(1,128)S(1)} %collective-permute-done.refs_1_, f32[1,1280]{1,0:T(1,128)S(1)} %collective-permute-done.2.refs_2_), custom_call_target="tpu_custom_call" | custom-call | tf_op jit(solution)/shard_map/pallas_call | solution.py:206
  (5 shorter events, 0.1 us)
Async XLA Ops:
  0.0 32.4 %slice-start = ((s8[20971520]{0:T(1024)(128)(4,1)}), s8[4194304]{0:T(1024)(128)(4,1)S(1)}, s32[]{:S(2)}) async-start(s8[20971520]{0:T(1024)(128)(4,1)} %bitcast.6), calls=%async_computation.2 | async-start | bytes 8388608
  0.0 0.8 %copy-start.3 = (bf16[1,2,8,128]{3,2,1,0:T(8,128)(2,1)S(1)}, bf16[1,2,8,128]{3,2,1,0:T(8,128)(2,1)}, u32[]{:S(2)}) copy-start(bf16[1,2,8,128]{3,2,1,0:T(8,128)(2,1)} %param.5) | copy-start | bytes 12292
  0.8 16.2 %copy-start = (bf16[32,2,512,128]{3,2,1,0:T(8,128)(2,1)S(1)}, bf16[32,2,512,128]{3,2,1,0:T(8,128)(2,1)}, u32[]{:S(2)}) copy-start(bf16[32,2,512,128]{3,2,1,0:T(8,128)(2,1)} %key_ref.1) | copy-start | bytes 25165828
  0.8 16.2 %copy-start.1 = (bf16[32,2,512,128]{3,2,1,0:T(8,128)(2,1)S(1)}, bf16[32,2,512,128]{3,2,1,0:T(8,128)(2,1)}, u32[]{:S(2)}) copy-start(bf16[32,2,512,128]{3,2,1,0:T(8,128)(2,1)} %value_ref.1) | copy-start | bytes 25165828
  0.8 16.2 %copy-start.2 = (s32[32]{0:T(128)S(1)}, s32[32]{0:T(128)}, u32[]{:S(2)}) copy-start(s32[32]{0:T(128)} %param.8) | copy-start | bytes 388
  0.8 31.6 %slice-start.1 = ((s8[20971520]{0:T(1024)(128)(4,1)}), s8[4194304]{0:T(1024)(128)(4,1)S(1)}, s32[]{:S(2)}) async-start(s8[20971520]{0:T(1024)(128)(4,1)} %bitcast.6), calls=%async_computation.3 | async-start | bytes 8388608
  0.9 31.6 %slice-start.2 = ((s8[20971520]{0:T(1024)(128)(4,1)}), s8[4194304]{0:T(1024)(128)(4,1)S(1)}, s32[]{:S(2)}) async-start(s8[20971520]{0:T(1024)(128)(4,1)} %bitcast.6), calls=%async_computation.4 | async-start | bytes 8388608
  0.9 31.6 %slice-start.3 = ((s8[20971520]{0:T(1024)(128)(4,1)}), s8[4194304]{0:T(1024)(128)(4,1)S(1)}, s32[]{:S(2)}) async-start(s8[20971520]{0:T(1024)(128)(4,1)} %bitcast.6), calls=%async_computation.5 | async-start | bytes 8388608
  0.9 31.6 %slice-start.4 = ((s8[20971520]{0:T(1024)(128)(4,1)}), s8[4194304]{0:T(1024)(128)(4,1)S(1)}, s32[]{:S(2)}) async-start(s8[20971520]{0:T(1024)(128)(4,1)} %bitcast.6), calls=%async_computation.6 | async-start | bytes 8388608
  34.5 3.7 %collective-permute-start.1 = (f32[1,1280]{1,0:T(1,128)S(1)}, f32[1,1280]{1,0:T(1,128)S(1)}, u32[]{:S(2)}, u32[]{:S(2)}) collective-permute-start(f32[1,1280]{1,0:T(1,128)S(1)} %get-tuple-element.8), channel_id=1, source_target_pairs={{0,1},{1,0},{2,3},{3,2},{4,5},{5,4},{6,7},{7,6},{8,9},{9,8},{10,11... | collective-permute-start | bytes 15368 | tf_op jit(solution)/shard_map/ppermute | solution.py:192
  37.0 5.1 %collective-permute-start = (f32[1,1280]{1,0:T(1,128)S(1)}, f32[1,1280]{1,0:T(1,128)S(1)}, u32[]{:S(2)}, u32[]{:S(2)}) collective-permute-start(f32[1,1280]{1,0:T(1,128)S(1)} %project_next.4), channel_id=1, source_target_pairs={{0,1},{1,0},{2,3},{3,2},{4,5},{5,4},{6,7},{7,6},{8,9},{9,8},{10,11... | collective-permute-start | bytes 15368 | tf_op jit(solution)/shard_map/ppermute | solution.py:192
  38.2 4.8 %collective-permute-start.2 = (f32[1,1280]{1,0:T(1,128)S(1)}, f32[1,1280]{1,0:T(1,128)S(1)}, u32[]{:S(2)}, u32[]{:S(2)}) collective-permute-start(f32[1,1280]{1,0:T(1,128)S(1)} %shard_map.55), channel_id=1, source_target_pairs={{0,3},{1,2},{2,1},{3,0},{4,7},{5,6},{6,5},{7,4},{8,11},{9,10},{10,... | collective-permute-start | bytes 15368 | tf_op jit(solution)/shard_map/ppermute | solution.py:192

commit v8 on v7

--- a/solution.py
+++ b/solution.py
@@ -10,7 +10,8 @@
 HEAD_SIZE = 128
 EMPTY = -4000.0
 TINY = 1e-30
-SPAN = 16384.0
+SPAN = 28.99
+LOWEST = -13.0
 LOG2_E = 1.4426950408889634
 STEP = 256
 NEAR, LAST = 1, 3
@@ -27,6 +28,20 @@
     second = jnp.floor(x * 2.0**9 + 0.5)
     x = x - second * 2.0**-9
     return first, second, jnp.floor(x * 2.0**20 + 0.5)
+
+
+def encode(x):
+    size = jnp.abs(x)
+    whole = jnp.floor(size)
+    code = jnp.exp2(whole + LOWEST) * (1.0 + (size - whole))
+    return jnp.where(x < 0.0, -code, code)
+
+
+def decode(code):
+    size = jnp.abs(code)
+    power = jnp.floor(log2(size))
+    x = power - LOWEST + (size * jnp.exp2(-power) - 1.0)
+    return jnp.where(code < 0.0, -x, x)
 
 
 def attend(used_ref, query_ref, key_ref, value_ref, out_ref):
@@ -78,7 +93,7 @@
             axis=0,
         )
         largest = jnp.maximum(jnp.max(jnp.abs(read), axis=1, keepdims=True), TINY)
-        out_ref[pl.ds(b * (rows + 2), rows), :] = read * (SPAN / largest)
+        out_ref[pl.ds(b * (rows + 2), rows), :] = encode(read * (SPAN / largest))
         pieces = split(top + log2(largest / SPAN)) + split(top + log2(jnp.maximum(total, TINY)))
         stats = jnp.zeros((rows, HEAD_SIZE), jnp.float32)
         for i, piece in enumerate(pieces):
@@ -107,7 +122,8 @@
     scale = jnp.exp2(tops - most) / jnp.sum(jnp.exp2(sums - most), axis=0, keepdims=True)
     scale = jnp.transpose(scale)[:rows]
     terms = [
-        arrived_ref[pl.ds(s * (rows + 2), rows), :] * scale[:, s : s + 1] for s in range(sources)
+        decode(arrived_ref[pl.ds(s * (rows + 2), rows), :]) * scale[:, s : s + 1]
+        for s in range(sources)
     ]
     while len(terms) > 1:
         terms = [a + b for a, b in zip(terms[::2], terms[1::2])]

time: 43.8 us -> 43.9 us (level)
  no operation moved by 1% of the time
where the time goes in v8:
time: 43.9 us; the launch traced here: 43.7 us
  blocking collectives  27.5 us (63%)
  Pallas kernels  8.26 us (19%)
  starting transfers between devices  5.2 us (12%)
  waiting for transfers between devices  1.7 us (4%)
  local copies, waits for them, and re-layouts  0.87 us (2%)
    all_to_all x1, blocking collectives, per_device(): lax.all_to_all(copies, 'seq', split_axis=0, concat_axis=0, tiled=True)  16.1 us
    all_to_all x1, blocking collectives, per_device(): lax.all_to_all(halves, 'seq', split_axis=0, concat_axis=0, tiled=True)  11.4 us
    ppermute x3, starting transfers between devices, send(): return lax.ppermute(term, 'group', [(j, j ^ away) for j in range(shares)])  5.2 us
    pallas_call x1, Pallas kernels, per_device(): pl.pallas_call(attend, out_shape=jax.ShapeDtypeStruct((batch * (rows + 2)...  3.97 us
    pallas_call x3, Pallas kernels, following(): pl.pallas_call(functools.partial(project_next, away), out_shape=piece, in...  2.43 us
    ppermute x3, waiting for transfers between devices, send(): return lax.ppermute(term, 'group', [(j, j ^ away) for j in range(shares)])  1.7 us
    pallas_call x1, Pallas kernels, per_device(): pl.pallas_call(functools.partial(project_first, NEAR ^ LAST), out_shape=(...  1.23 us
  transfers between devices with their start and end apart: 3, of which 2 were waited for; matrix products, arithmetic and copies ran while one was open for 0% of the time, Pallas kernels for 4%

profile of v8, /device:TPU:0, one launch (start us, length us, event | category | flops | bytes accessed | tf_op | source)
XLA Modules:
  0.0 43.7 jit_solution(3227608175248874346)
XLA Ops:
  0.0 0.0 slice-start
  0.0 0.0 copy-start.3
  0.0 0.8 %copy-done.3 = bf16[1,2,8,128]{3,2,1,0:T(8,128)(2,1)S(1)} copy-done((bf16[1,2,8,128]{3,2,1,0:T(8,128)(2,1)S(1)}, bf16[1,2,8,128]{3,2,1,0:T(8,128)(2,1)}, u32[]{:S(2)}) %copy-start.3) | copy-done | bytes 4120
  0.8 0.0 copy-start
  0.8 0.0 copy-start.1
  0.8 0.0 copy-start.2
  0.8 0.0 slice-start.1
  0.9 0.0 slice-start.2
  0.9 0.0 slice-start.3
  0.9 0.0 slice-start.4
  0.9 16.1 %all_to_all.10.query_ref = bf16[32,16,128]{2,1,0:T(8,128)(2,1)S(1)} all-to-all(bf16[32,16,128]{2,1,0:T(8,128)(2,1)S(1)} %spread.1), channel_id=1, replica_groups=mesh['seq'=32,'group'=4] {'seq'}, dimensions={0} | all-to-all | bytes 262144 | tf_op jit(solution)/shard_map/all_to_all | solution.py:181
  17.0 0.0 copy-done
  17.0 0.0 copy-done.1
  17.0 0.0 copy-done.2
  17.0 4.0 %attend.1 = f32[576,128]{1,0:T(8,128)S(1)} custom-call(s32[1,32]{1,0:T(1,128)S(1)} %bitcast.12, bf16[32,16,128]{2,1,0:T(8,128)(2,1)S(1)} %all_to_all.10.query_ref, bf16[32,2,512,128]{3,2,1,0:T(8,128)(2,1)S(1)} %copy-done, bf16[32,2,512,128]{3,2,1,0:T(8,128)(2,1)S(1)} %copy-done.1), custom_call_target="tpu_custom_call" | custom-call | tf_op jit(solution)/shard_map/attend/pallas_call | solution.py:182
  21.0 11.4 %all_to_all.11 = f16[32,9,2,128]{3,2,1,0:T(2,128)(2,1)S(1)} all-to-all(f16[32,9,2,128]{3,2,1,0:T(2,128)(2,1)S(1)} %bitcast.14), channel_id=1, replica_groups=mesh['seq'=32,'group'=4] {'seq'}, dimensions={0} | all-to-all | bytes 294912 | tf_op jit(solution)/shard_map/all_to_all | solution.py:191
  32.4 0.0 slice-done
  32.5 0.0 slice-done.1
  32.5 0.0 slice-done.2
  32.5 0.0 slice-done.3
  32.5 0.0 slice-done.4
  32.5 1.2 %project_first.1 = (bf16[16,2048]{1,0:T(8,128)(2,1)S(1)}, f32[1,1280]{1,0:T(1,128)S(1)}) custom-call(f32[576,128]{1,0:T(8,128)S(1)} %convert.1.arrived_ref, bf16[2048,5120]{1,0:T(8,128)(2,1)S(1)} %bitcast.8), custom_call_target="tpu_custom_call" | custom-call | tf_op jit(solution)/shard_map/project_first/pallas_call | solution.py:198
  33.7 0.8 %project_next.5.refs_0_ = f32[1,1280]{1,0:T(1,128)S(1)} custom-call(bf16[16,2048]{1,0:T(8,128)(2,1)S(1)} %get-tuple-element.7.left_ref, bf16[2048,5120]{1,0:T(8,128)(2,1)S(1)} %bitcast.9), custom_call_target="tpu_custom_call" | custom-call | flops 1000000000 | bytes 10000000 | tf_op jit(solution)/shard_map/project_next/pallas_call | solution.py:211
  34.6 1.7 %collective-permute-start.1 = (f32[1,1280]{1,0:T(1,128)S(1)}, f32[1,1280]{1,0:T(1,128)S(1)}, u32[]{:S(2)}, u32[]{:S(2)}) collective-permute-start(f32[1,1280]{1,0:T(1,128)S(1)} %get-tuple-element.8), channel_id=1, source_target_pairs={{0,1},{1,0},{2,3},{3,2},{4,5},{5,4},{6,7},{7,6},{8,9},{9,8},{10,11... | collective-permute-start | bytes 15368 | tf_op jit(solution)/shard_map/ppermute | solution.py:208
  36.2 0.8 %project_next.4 = f32[1,1280]{1,0:T(1,128)S(1)} custom-call(bf16[16,2048]{1,0:T(8,128)(2,1)S(1)} %get-tuple-element.7.left_ref, bf16[2048,5120]{1,0:T(8,128)(2,1)S(1)} %bitcast.10), custom_call_target="tpu_custom_call" | custom-call | flops 1000000000 | bytes 10000000 | tf_op jit(solution)/shard_map/project_next/pallas_call | solution.py:211
  37.0 0.5 %collective-permute-start = (f32[1,1280]{1,0:T(1,128)S(1)}, f32[1,1280]{1,0:T(1,128)S(1)}, u32[]{:S(2)}, u32[]{:S(2)}) collective-permute-start(f32[1,1280]{1,0:T(1,128)S(1)} %project_next.4), channel_id=1, source_target_pairs={{0,1},{1,0},{2,3},{3,2},{4,5},{5,4},{6,7},{7,6},{8,9},{9,8},{10,11... | collective-permute-start | bytes 15368 | tf_op jit(solution)/shard_map/ppermute | solution.py:208
  37.6 0.7 %collective-permute-done.1.refs_1_ = f32[1,1280]{1,0:T(1,128)S(1)} collective-permute-done((f32[1,1280]{1,0:T(1,128)S(1)}, f32[1,1280]{1,0:T(1,128)S(1)}, u32[]{:S(2)}, u32[]{:S(2)}) %collective-permute-start.1) | collective-permute-done | bytes 5152 | tf_op jit(solution)/shard_map/ppermute | solution.py:208
  38.3 3.0 %collective-permute-start.2 = (f32[1,1280]{1,0:T(1,128)S(1)}, f32[1,1280]{1,0:T(1,128)S(1)}, u32[]{:S(2)}, u32[]{:S(2)}) collective-permute-start(f32[1,1280]{1,0:T(1,128)S(1)} %shard_map.55), channel_id=1, source_target_pairs={{0,3},{1,2},{2,1},{3,0},{4,7},{5,6},{6,5},{7,4},{8,11},{9,10},{10,... | collective-permute-start | bytes 15368 | tf_op jit(solution)/shard_map/ppermute | solution.py:208
  41.3 0.8 %project_next.3.refs_0_ = f32[1,1280]{1,0:T(1,128)S(1)} custom-call(bf16[16,2048]{1,0:T(8,128)(2,1)S(1)} %get-tuple-element.7.left_ref, bf16[2048,5120]{1,0:T(8,128)(2,1)S(1)} %bitcast.11), custom_call_target="tpu_custom_call" | custom-call | flops 1000000000 | bytes 10000000 | tf_op jit(solution)/shard_map/project_next/pallas_call | solution.py:211
  42.1 0.0 collective-permute-done.refs_1_
  42.1 1.0 %collective-permute-done.2.refs_2_ = f32[1,1280]{1,0:T(1,128)S(1)} collective-permute-done((f32[1,1280]{1,0:T(1,128)S(1)}, f32[1,1280]{1,0:T(1,128)S(1)}, u32[]{:S(2)}, u32[]{:S(2)}) %collective-permute-start.2) | collective-permute-done | bytes 5152 | tf_op jit(solution)/shard_map/ppermute | solution.py:208
  43.1 0.6 %shard_map.56 = bf16[1,1280]{1,0:T(2,128)(2,1)} custom-call(f32[1,1280]{1,0:T(1,128)S(1)} %project_next.3.refs_0_, f32[1,1280]{1,0:T(1,128)S(1)} %collective-permute-done.refs_1_, f32[1,1280]{1,0:T(1,128)S(1)} %collective-permute-done.2.refs_2_), custom_call_target="tpu_custom_call" | custom-call | tf_op jit(solution)/shard_map/pallas_call | solution.py:222
  (5 shorter events, 0.1 us)
Async XLA Ops:
  0.0 32.4 %slice-start = ((s8[20971520]{0:T(1024)(128)(4,1)}), s8[4194304]{0:T(1024)(128)(4,1)S(1)}, s32[]{:S(2)}) async-start(s8[20971520]{0:T(1024)(128)(4,1)} %bitcast.6), calls=%async_computation.2 | async-start | bytes 8388608
  0.0 0.8 %copy-start.3 = (bf16[1,2,8,128]{3,2,1,0:T(8,128)(2,1)S(1)}, bf16[1,2,8,128]{3,2,1,0:T(8,128)(2,1)}, u32[]{:S(2)}) copy-start(bf16[1,2,8,128]{3,2,1,0:T(8,128)(2,1)} %param.5) | copy-start | bytes 12292
  0.8 16.2 %copy-start = (bf16[32,2,512,128]{3,2,1,0:T(8,128)(2,1)S(1)}, bf16[32,2,512,128]{3,2,1,0:T(8,128)(2,1)}, u32[]{:S(2)}) copy-start(bf16[32,2,512,128]{3,2,1,0:T(8,128)(2,1)} %key_ref.1) | copy-start | bytes 25165828
  0.8 16.2 %copy-start.1 = (bf16[32,2,512,128]{3,2,1,0:T(8,128)(2,1)S(1)}, bf16[32,2,512,128]{3,2,1,0:T(8,128)(2,1)}, u32[]{:S(2)}) copy-start(bf16[32,2,512,128]{3,2,1,0:T(8,128)(2,1)} %value_ref.1) | copy-start | bytes 25165828
  0.8 16.2 %copy-start.2 = (s32[32]{0:T(128)S(1)}, s32[32]{0:T(128)}, u32[]{:S(2)}) copy-start(s32[32]{0:T(128)} %param.8) | copy-start | bytes 388
  0.8 31.6 %slice-start.1 = ((s8[20971520]{0:T(1024)(128)(4,1)}), s8[4194304]{0:T(1024)(128)(4,1)S(1)}, s32[]{:S(2)}) async-start(s8[20971520]{0:T(1024)(128)(4,1)} %bitcast.6), calls=%async_computation.3 | async-start | bytes 8388608
  0.9 31.6 %slice-start.2 = ((s8[20971520]{0:T(1024)(128)(4,1)}), s8[4194304]{0:T(1024)(128)(4,1)S(1)}, s32[]{:S(2)}) async-start(s8[20971520]{0:T(1024)(128)(4,1)} %bitcast.6), calls=%async_computation.4 | async-start | bytes 8388608
  0.9 31.6 %slice-start.3 = ((s8[20971520]{0:T(1024)(128)(4,1)}), s8[4194304]{0:T(1024)(128)(4,1)S(1)}, s32[]{:S(2)}) async-start(s8[20971520]{0:T(1024)(128)(4,1)} %bitcast.6), calls=%async_computation.5 | async-start | bytes 8388608
  0.9 31.6 %slice-start.4 = ((s8[20971520]{0:T(1024)(128)(4,1)}), s8[4194304]{0:T(1024)(128)(4,1)S(1)}, s32[]{:S(2)}) async-start(s8[20971520]{0:T(1024)(128)(4,1)} %bitcast.6), calls=%async_computation.6 | async-start | bytes 8388608
  34.6 3.7 %collective-permute-start.1 = (f32[1,1280]{1,0:T(1,128)S(1)}, f32[1,1280]{1,0:T(1,128)S(1)}, u32[]{:S(2)}, u32[]{:S(2)}) collective-permute-start(f32[1,1280]{1,0:T(1,128)S(1)} %get-tuple-element.8), channel_id=1, source_target_pairs={{0,1},{1,0},{2,3},{3,2},{4,5},{5,4},{6,7},{7,6},{8,9},{9,8},{10,11... | collective-permute-start | bytes 15368 | tf_op jit(solution)/shard_map/ppermute | solution.py:208
  37.0 5.1 %collective-permute-start = (f32[1,1280]{1,0:T(1,128)S(1)}, f32[1,1280]{1,0:T(1,128)S(1)}, u32[]{:S(2)}, u32[]{:S(2)}) collective-permute-start(f32[1,1280]{1,0:T(1,128)S(1)} %project_next.4), channel_id=1, source_target_pairs={{0,1},{1,0},{2,3},{3,2},{4,5},{5,4},{6,7},{7,6},{8,9},{9,8},{10,11... | collective-permute-start | bytes 15368 | tf_op jit(solution)/shard_map/ppermute | solution.py:208
  38.3 4.8 %collective-permute-start.2 = (f32[1,1280]{1,0:T(1,128)S(1)}, f32[1,1280]{1,0:T(1,128)S(1)}, u32[]{:S(2)}, u32[]{:S(2)}) collective-permute-start(f32[1,1280]{1,0:T(1,128)S(1)} %shard_map.55), channel_id=1, source_target_pairs={{0,3},{1,2},{2,1},{3,0},{4,7},{5,6},{6,5},{7,4},{8,11},{9,10},{10,... | collective-permute-start | bytes 15368 | tf_op jit(solution)/shard_map/ppermute | solution.py:208

commit v9 on v8

--- a/solution.py
+++ b/solution.py
@@ -72,19 +72,17 @@
         )
     filled = [place < used[:, b : b + 1] for b in at]
     logits = [jnp.where(f, x * TO_BASE_2, EMPTY) for f, x in zip(filled, logits)]
-    tops = [jnp.max(x, axis=1, keepdims=True) for x in logits]
-    parts = [jnp.where(f, jnp.exp2(x - t), 0.0) for f, x, t in zip(filled, logits, tops)]
+    tops = [jnp.maximum(jnp.max(x, axis=1, keepdims=True), 0.5 * EMPTY) for x in logits]
+    parts = [jnp.exp2(x - t) for x, t in zip(logits, tops)]
     totals = [jnp.sum(p, axis=1, keepdims=True) for p in parts]
-    reads = []
-    for b, part in zip(at, parts):
+    for b, part, top, total in zip(at, parts, tops, totals):
         high = part.astype(jnp.bfloat16)
         low = (part - high.astype(jnp.float32)).astype(jnp.bfloat16)
         both = jnp.dot(
             jnp.concatenate([high, low], axis=0), side_by_side(value_ref, b),
             preferred_element_type=jnp.float32,
         )
-        reads.append(both[:rows] + both[rows:])
-    for b, read, top, total in zip(at, reads, tops, totals):
+        read = both[:rows] + both[rows:]
         read = jnp.concatenate(
             [
                 read[k * group : (k + 1) * group, k * HEAD_SIZE : (k + 1) * HEAD_SIZE]

time: 43.9 us -> 43.9 us (level)
  no operation moved by 1% of the time
where the time goes in v9:
time: 43.9 us; the launch traced here: 43.7 us
  blocking collectives  27.5 us (63%)
  Pallas kernels  8.26 us (19%)
  starting transfers between devices  5.2 us (12%)
  waiting for transfers between devices  1.7 us (4%)
  local copies, waits for them, and re-layouts  0.87 us (2%)
    all_to_all x1, blocking collectives, per_device(): lax.all_to_all(copies, 'seq', split_axis=0, concat_axis=0, tiled=True)  16.1 us
    all_to_all x1, blocking collectives, per_device(): lax.all_to_all(halves, 'seq', split_axis=0, concat_axis=0, tiled=True)  11.4 us
    ppermute x3, starting transfers between devices, send(): return lax.ppermute(term, 'group', [(j, j ^ away) for j in range(shares)])  5.2 us
    pallas_call x1, Pallas kernels, per_device(): pl.pallas_call(attend, out_shape=jax.ShapeDtypeStruct((batch * (rows + 2)...  3.97 us
    pallas_call x3, Pallas kernels, following(): pl.pallas_call(functools.partial(project_next, away), out_shape=piece, in...  2.43 us
    ppermute x3, waiting for transfers between devices, send(): return lax.ppermute(term, 'group', [(j, j ^ away) for j in range(shares)])  1.7 us
    pallas_call x1, Pallas kernels, per_device(): pl.pallas_call(functools.partial(project_first, NEAR ^ LAST), out_shape=(...  1.23 us
  transfers between devices with their start and end apart: 3, of which 2 were waited for; matrix products, arithmetic and copies ran while one was open for 0% of the time, Pallas kernels for 4%

profile of v9, /device:TPU:0, one launch (start us, length us, event | category | flops | bytes accessed | tf_op | source)
XLA Modules:
  0.0 43.7 jit_solution(15385448715627653886)
XLA Ops:
  0.0 0.0 slice-start
  0.0 0.0 copy-start.3
  0.0 0.8 %copy-done.3 = bf16[1,2,8,128]{3,2,1,0:T(8,128)(2,1)S(1)} copy-done((bf16[1,2,8,128]{3,2,1,0:T(8,128)(2,1)S(1)}, bf16[1,2,8,128]{3,2,1,0:T(8,128)(2,1)}, u32[]{:S(2)}) %copy-start.3) | copy-done | bytes 4120
  0.8 0.0 copy-start
  0.8 0.0 copy-start.1
  0.8 0.0 copy-start.2
  0.8 0.0 slice-start.1
  0.9 0.0 slice-start.2
  0.9 0.0 slice-start.3
  0.9 0.0 slice-start.4
  0.9 16.1 %all_to_all.10.query_ref = bf16[32,16,128]{2,1,0:T(8,128)(2,1)S(1)} all-to-all(bf16[32,16,128]{2,1,0:T(8,128)(2,1)S(1)} %spread.1), channel_id=1, replica_groups=mesh['seq'=32,'group'=4] {'seq'}, dimensions={0} | all-to-all | bytes 262144 | tf_op jit(solution)/shard_map/all_to_all | solution.py:179
  17.0 0.0 copy-done
  17.0 0.0 copy-done.1
  17.0 0.0 copy-done.2
  17.0 4.0 %attend.1 = f32[576,128]{1,0:T(8,128)S(1)} custom-call(s32[1,32]{1,0:T(1,128)S(1)} %bitcast.12, bf16[32,16,128]{2,1,0:T(8,128)(2,1)S(1)} %all_to_all.10.query_ref, bf16[32,2,512,128]{3,2,1,0:T(8,128)(2,1)S(1)} %copy-done, bf16[32,2,512,128]{3,2,1,0:T(8,128)(2,1)S(1)} %copy-done.1), custom_call_target="tpu_custom_call" | custom-call | tf_op jit(solution)/shard_map/attend/pallas_call | solution.py:180
  21.0 11.4 %all_to_all.11 = f16[32,9,2,128]{3,2,1,0:T(2,128)(2,1)S(1)} all-to-all(f16[32,9,2,128]{3,2,1,0:T(2,128)(2,1)S(1)} %bitcast.14), channel_id=1, replica_groups=mesh['seq'=32,'group'=4] {'seq'}, dimensions={0} | all-to-all | bytes 294912 | tf_op jit(solution)/shard_map/all_to_all | solution.py:189
  32.4 0.0 slice-done
  32.5 0.0 slice-done.1
  32.5 0.0 slice-done.2
  32.5 0.0 slice-done.3
  32.5 0.0 slice-done.4
  32.5 1.2 %project_first.1 = (bf16[16,2048]{1,0:T(8,128)(2,1)S(1)}, f32[1,1280]{1,0:T(1,128)S(1)}) custom-call(f32[576,128]{1,0:T(8,128)S(1)} %convert.1.arrived_ref, bf16[2048,5120]{1,0:T(8,128)(2,1)S(1)} %bitcast.8), custom_call_target="tpu_custom_call" | custom-call | tf_op jit(solution)/shard_map/project_first/pallas_call | solution.py:196
  33.7 0.8 %project_next.5.refs_0_ = f32[1,1280]{1,0:T(1,128)S(1)} custom-call(bf16[16,2048]{1,0:T(8,128)(2,1)S(1)} %get-tuple-element.7.left_ref, bf16[2048,5120]{1,0:T(8,128)(2,1)S(1)} %bitcast.9), custom_call_target="tpu_custom_call" | custom-call | flops 1000000000 | bytes 10000000 | tf_op jit(solution)/shard_map/project_next/pallas_call | solution.py:209
  34.6 1.7 %collective-permute-start.1 = (f32[1,1280]{1,0:T(1,128)S(1)}, f32[1,1280]{1,0:T(1,128)S(1)}, u32[]{:S(2)}, u32[]{:S(2)}) collective-permute-start(f32[1,1280]{1,0:T(1,128)S(1)} %get-tuple-element.8), channel_id=1, source_target_pairs={{0,1},{1,0},{2,3},{3,2},{4,5},{5,4},{6,7},{7,6},{8,9},{9,8},{10,11... | collective-permute-start | bytes 15368 | tf_op jit(solution)/shard_map/ppermute | solution.py:206
  36.2 0.8 %project_next.4 = f32[1,1280]{1,0:T(1,128)S(1)} custom-call(bf16[16,2048]{1,0:T(8,128)(2,1)S(1)} %get-tuple-element.7.left_ref, bf16[2048,5120]{1,0:T(8,128)(2,1)S(1)} %bitcast.10), custom_call_target="tpu_custom_call" | custom-call | flops 1000000000 | bytes 10000000 | tf_op jit(solution)/shard_map/project_next/pallas_call | solution.py:209
  37.0 0.5 %collective-permute-start = (f32[1,1280]{1,0:T(1,128)S(1)}, f32[1,1280]{1,0:T(1,128)S(1)}, u32[]{:S(2)}, u32[]{:S(2)}) collective-permute-start(f32[1,1280]{1,0:T(1,128)S(1)} %project_next.4), channel_id=1, source_target_pairs={{0,1},{1,0},{2,3},{3,2},{4,5},{5,4},{6,7},{7,6},{8,9},{9,8},{10,11... | collective-permute-start | bytes 15368 | tf_op jit(solution)/shard_map/ppermute | solution.py:206
  37.6 0.7 %collective-permute-done.1.refs_1_ = f32[1,1280]{1,0:T(1,128)S(1)} collective-permute-done((f32[1,1280]{1,0:T(1,128)S(1)}, f32[1,1280]{1,0:T(1,128)S(1)}, u32[]{:S(2)}, u32[]{:S(2)}) %collective-permute-start.1) | collective-permute-done | bytes 5152 | tf_op jit(solution)/shard_map/ppermute | solution.py:206
  38.3 3.0 %collective-permute-start.2 = (f32[1,1280]{1,0:T(1,128)S(1)}, f32[1,1280]{1,0:T(1,128)S(1)}, u32[]{:S(2)}, u32[]{:S(2)}) collective-permute-start(f32[1,1280]{1,0:T(1,128)S(1)} %shard_map.55), channel_id=1, source_target_pairs={{0,3},{1,2},{2,1},{3,0},{4,7},{5,6},{6,5},{7,4},{8,11},{9,10},{10,... | collective-permute-start | bytes 15368 | tf_op jit(solution)/shard_map/ppermute | solution.py:206
  41.3 0.8 %project_next.3.refs_0_ = f32[1,1280]{1,0:T(1,128)S(1)} custom-call(bf16[16,2048]{1,0:T(8,128)(2,1)S(1)} %get-tuple-element.7.left_ref, bf16[2048,5120]{1,0:T(8,128)(2,1)S(1)} %bitcast.11), custom_call_target="tpu_custom_call" | custom-call | flops 1000000000 | bytes 10000000 | tf_op jit(solution)/shard_map/project_next/pallas_call | solution.py:209
  42.1 0.0 collective-permute-done.refs_1_
  42.1 1.0 %collective-permute-done.2.refs_2_ = f32[1,1280]{1,0:T(1,128)S(1)} collective-permute-done((f32[1,1280]{1,0:T(1,128)S(1)}, f32[1,1280]{1,0:T(1,128)S(1)}, u32[]{:S(2)}, u32[]{:S(2)}) %collective-permute-start.2) | collective-permute-done | bytes 5152 | tf_op jit(solution)/shard_map/ppermute | solution.py:206
  43.1 0.6 %shard_map.56 = bf16[1,1280]{1,0:T(2,128)(2,1)} custom-call(f32[1,1280]{1,0:T(1,128)S(1)} %project_next.3.refs_0_, f32[1,1280]{1,0:T(1,128)S(1)} %collective-permute-done.refs_1_, f32[1,1280]{1,0:T(1,128)S(1)} %collective-permute-done.2.refs_2_), custom_call_target="tpu_custom_call" | custom-call | tf_op jit(solution)/shard_map/pallas_call | solution.py:220
  (5 shorter events, 0.1 us)
Async XLA Ops:
  0.0 32.4 %slice-start = ((s8[20971520]{0:T(1024)(128)(4,1)}), s8[4194304]{0:T(1024)(128)(4,1)S(1)}, s32[]{:S(2)}) async-start(s8[20971520]{0:T(1024)(128)(4,1)} %bitcast.6), calls=%async_computation.2 | async-start | bytes 8388608
  0.0 0.8 %copy-start.3 = (bf16[1,2,8,128]{3,2,1,0:T(8,128)(2,1)S(1)}, bf16[1,2,8,128]{3,2,1,0:T(8,128)(2,1)}, u32[]{:S(2)}) copy-start(bf16[1,2,8,128]{3,2,1,0:T(8,128)(2,1)} %param.5) | copy-start | bytes 12292
  0.8 16.2 %copy-start = (bf16[32,2,512,128]{3,2,1,0:T(8,128)(2,1)S(1)}, bf16[32,2,512,128]{3,2,1,0:T(8,128)(2,1)}, u32[]{:S(2)}) copy-start(bf16[32,2,512,128]{3,2,1,0:T(8,128)(2,1)} %key_ref.1) | copy-start | bytes 25165828
  0.8 16.2 %copy-start.1 = (bf16[32,2,512,128]{3,2,1,0:T(8,128)(2,1)S(1)}, bf16[32,2,512,128]{3,2,1,0:T(8,128)(2,1)}, u32[]{:S(2)}) copy-start(bf16[32,2,512,128]{3,2,1,0:T(8,128)(2,1)} %value_ref.1) | copy-start | bytes 25165828
  0.8 16.2 %copy-start.2 = (s32[32]{0:T(128)S(1)}, s32[32]{0:T(128)}, u32[]{:S(2)}) copy-start(s32[32]{0:T(128)} %param.8) | copy-start | bytes 388
  0.8 31.6 %slice-start.1 = ((s8[20971520]{0:T(1024)(128)(4,1)}), s8[4194304]{0:T(1024)(128)(4,1)S(1)}, s32[]{:S(2)}) async-start(s8[20971520]{0:T(1024)(128)(4,1)} %bitcast.6), calls=%async_computation.3 | async-start | bytes 8388608
  0.9 31.6 %slice-start.2 = ((s8[20971520]{0:T(1024)(128)(4,1)}), s8[4194304]{0:T(1024)(128)(4,1)S(1)}, s32[]{:S(2)}) async-start(s8[20971520]{0:T(1024)(128)(4,1)} %bitcast.6), calls=%async_computation.4 | async-start | bytes 8388608
  0.9 31.6 %slice-start.3 = ((s8[20971520]{0:T(1024)(128)(4,1)}), s8[4194304]{0:T(1024)(128)(4,1)S(1)}, s32[]{:S(2)}) async-start(s8[20971520]{0:T(1024)(128)(4,1)} %bitcast.6), calls=%async_computation.5 | async-start | bytes 8388608
  0.9 31.6 %slice-start.4 = ((s8[20971520]{0:T(1024)(128)(4,1)}), s8[4194304]{0:T(1024)(128)(4,1)S(1)}, s32[]{:S(2)}) async-start(s8[20971520]{0:T(1024)(128)(4,1)} %bitcast.6), calls=%async_computation.6 | async-start | bytes 8388608
  34.6 3.7 %collective-permute-start.1 = (f32[1,1280]{1,0:T(1,128)S(1)}, f32[1,1280]{1,0:T(1,128)S(1)}, u32[]{:S(2)}, u32[]{:S(2)}) collective-permute-start(f32[1,1280]{1,0:T(1,128)S(1)} %get-tuple-element.8), channel_id=1, source_target_pairs={{0,1},{1,0},{2,3},{3,2},{4,5},{5,4},{6,7},{7,6},{8,9},{9,8},{10,11... | collective-permute-start | bytes 15368 | tf_op jit(solution)/shard_map/ppermute | solution.py:206
  37.0 5.1 %collective-permute-start = (f32[1,1280]{1,0:T(1,128)S(1)}, f32[1,1280]{1,0:T(1,128)S(1)}, u32[]{:S(2)}, u32[]{:S(2)}) collective-permute-start(f32[1,1280]{1,0:T(1,128)S(1)} %project_next.4), channel_id=1, source_target_pairs={{0,1},{1,0},{2,3},{3,2},{4,5},{5,4},{6,7},{7,6},{8,9},{9,8},{10,11... | collective-permute-start | bytes 15368 | tf_op jit(solution)/shard_map/ppermute | solution.py:206
  38.3 4.8 %collective-permute-start.2 = (f32[1,1280]{1,0:T(1,128)S(1)}, f32[1,1280]{1,0:T(1,128)S(1)}, u32[]{:S(2)}, u32[]{:S(2)}) collective-permute-start(f32[1,1280]{1,0:T(1,128)S(1)} %shard_map.55), channel_id=1, source_target_pairs={{0,3},{1,2},{2,1},{3,0},{4,7},{5,6},{6,5},{7,4},{8,11},{9,10},{10,... | collective-permute-start | bytes 15368 | tf_op jit(solution)/shard_map/ppermute | solution.py:206
